TPU v7x, 32 devices: a 4x2x2 block of a 4x4x8 slice. The times are simulated.
32 devices in a mesh: dp: 4 (over y, z), tp: 8 (over x, core).
Axes of the slice: x: 4, y: 2, z: 2, core: 2. Of those that a mesh axis runs over, the one named last changes fastest.
The devices are a block of a 4x4x8 slice.
Arguments:
- x_tokens: bfloat16 [12, 384, 3072], P('dp', 'tp'), parts along dimension 0
- start_pos: int32 [12], P('dp'), parts along dimension 0
- k_cache: bfloat16 [2, 12, 8, 3456, 128], P(None, 'dp', 'tp'), parts along dimension 1
- v_cache: bfloat16 [2, 12, 8, 3456, 128], P(None, 'dp', 'tp'), parts along dimension 1
- w_q: bfloat16 [2, 3072, 4096], P(None, None, 'tp')
- w_k: bfloat16 [2, 3072, 1024], P(None, None, 'tp')
- w_v: bfloat16 [2, 3072, 1024], P(None, None, 'tp')
- w_o: bfloat16 [2, 4096, 3072], P(None, 'tp')
- w_up: bfloat16 [2, 3072, 9216], P(None, None, 'tp')
- w_down: bfloat16 [2, 9216, 3072], P(None, 'tp')
- ln_gain: bfloat16 [2, 2, 3072], replicated
- ln_bias: bfloat16 [2, 2, 3072], replicated
Outputs:
- output 1: bfloat16 [12, 384, 3072], P('dp', 'tp'), parts along dimension 0
- output 2: bfloat16 [2, 12, 8, 3456, 128], P(None, 'dp', 'tp'), parts along dimension 1
- output 3: bfloat16 [2, 12, 8, 3456, 128], P(None, 'dp', 'tp'), parts along dimension 1
There are 4 independent parts. A program takes and returns all parts, laid end to end along the dimension named above; an argument that names none is the same for every part.
All inputs are finite; a program needn't handle non-finite values.
Results may differ from a plain program's by a relative error of at most 0.02.
Values are sent between devices in bfloat16 or wider.
A program may use at most 768 MiB of HBM per device.

v0:
```python
import jax
import jax.numpy as jnp
from jax import lax
from jax.sharding import PartitionSpec as P

LN_EPS = 1e-5
ROPE_BASE = 10000.0
NEG_BIG = -1e30


def layer_norm1p(values_in, gain, bias):
    x_float = values_in.astype(jnp.float32)
    row_mean = jnp.mean(x_float, axis=-1, keepdims=True)
    centered = x_float - row_mean
    variance = jnp.mean(centered * centered, axis=-1, keepdims=True)
    normed = centered * lax.rsqrt(variance + LN_EPS)
    return (normed * (1.0 + gain.astype(jnp.float32)) + bias.astype(jnp.float32)).astype(jnp.bfloat16)


def rotate_half(values_in, positions):
    rot_dim = values_in.shape[-1] // 2
    half_rot = rot_dim // 2
    inv_freq = ROPE_BASE ** (-(jnp.arange(half_rot, dtype=jnp.float32) * (2.0 / rot_dim)))
    angles = positions.astype(jnp.float32)[..., None] * inv_freq
    cos_a = jnp.cos(angles)
    sin_a = jnp.sin(angles)
    first = values_in[..., :half_rot]
    second = values_in[..., half_rot:rot_dim]
    return jnp.concatenate([first * cos_a - second * sin_a, second * cos_a + first * sin_a, values_in[..., rot_dim:]], axis=-1)


def write_rows(cache_seq, new_rows, start_row):
    zero_idx = jnp.zeros_like(start_row)
    return lax.dynamic_update_slice(cache_seq, new_rows, (zero_idx, start_row, zero_idx))


def attention(q_rot, k_all, v_all, key_ok, scale):
    scores = jnp.einsum('bkgch,bksh->bkgcs', q_rot, k_all, preferred_element_type=jnp.float32) * scale
    scores = jnp.where(key_ok, scores, NEG_BIG)
    peak = jnp.max(scores, axis=-1, keepdims=True)
    weights = jnp.exp(scores - peak)
    row_sum = jnp.sum(weights, axis=-1, keepdims=True)
    context = jnp.einsum('bkgcs,bksh->bkgch', weights.astype(jnp.bfloat16), v_all, preferred_element_type=jnp.float32) / row_sum
    return context.astype(jnp.bfloat16)


def solution(mesh):
    tp_size = mesh.shape['tp']
    tok_spec = P('dp', 'tp', None)
    cache_spec = P(None, 'dp', 'tp', None, None)
    col_spec = P(None, None, 'tp')
    row_spec = P(None, 'tp', None)

    def device_fn(x_loc, start_pos, k_cache, v_cache, w_q, w_k, w_v, w_o, w_up, w_down, ln_gain, ln_bias):
        n_layers = w_q.shape[0]
        tok_loc = x_loc.shape[1]
        d_model = x_loc.shape[2]
        kv_loc = k_cache.shape[2]
        cache_len = k_cache.shape[3]
        head_dim = k_cache.shape[4]
        group_size = w_q.shape[2] // head_dim // kv_loc
        new_len = tok_loc * tp_size
        scale = head_dim ** -0.5
        positions = start_pos[:, None] + jnp.arange(new_len, dtype=jnp.int32)[None, :]
        key_ok = jnp.arange(cache_len, dtype=jnp.int32)[None, None, None, None, :] <= positions[:, None, None, :, None]
        hidden = x_loc
        k_list = []
        v_list = []
        for layer in range(n_layers):
            normed = layer_norm1p(hidden, ln_gain[layer, 0], ln_bias[layer, 0])
            normed_all = lax.all_gather(normed, 'tp', axis=1, tiled=True)
            q_proj = jnp.einsum('bcd,dkgh->bkgch', normed_all, w_q[layer].reshape(d_model, kv_loc, group_size, head_dim), preferred_element_type=jnp.float32)
            k_proj = jnp.einsum('bcd,dkh->bkch', normed_all, w_k[layer].reshape(d_model, kv_loc, head_dim), preferred_element_type=jnp.float32)
            v_rows = jnp.einsum('bcd,dkh->bkch', normed_all, w_v[layer].reshape(d_model, kv_loc, head_dim), preferred_element_type=jnp.float32).astype(jnp.bfloat16)
            q_rot = rotate_half(q_proj, positions[:, None, None, :]).astype(jnp.bfloat16)
            k_rows = rotate_half(k_proj, positions[:, None, :]).astype(jnp.bfloat16)
            k_new = jax.vmap(write_rows)(k_cache[layer], k_rows, start_pos)
            v_new = jax.vmap(write_rows)(v_cache[layer], v_rows, start_pos)
            context = attention(q_rot, k_new, v_new, key_ok, scale)
            attn_part = jnp.einsum('bkgch,kghd->bcd', context, w_o[layer].reshape(kv_loc, group_size, head_dim, d_model), preferred_element_type=jnp.float32).astype(jnp.bfloat16)
            attn_loc = lax.psum_scatter(attn_part, 'tp', scatter_dimension=1, tiled=True)
            after_attn = (hidden.astype(jnp.float32) + attn_loc.astype(jnp.float32)).astype(jnp.bfloat16)
            normed_mlp = layer_norm1p(after_attn, ln_gain[layer, 1], ln_bias[layer, 1])
            normed_mlp_all = lax.all_gather(normed_mlp, 'tp', axis=1, tiled=True)
            up_val = jnp.einsum('bcd,df->bcf', normed_mlp_all, w_up[layer], preferred_element_type=jnp.float32)
            act_sq = jnp.square(jnp.maximum(up_val, 0.0)).astype(jnp.bfloat16)
            mlp_part = jnp.einsum('bcf,fd->bcd', act_sq, w_down[layer], preferred_element_type=jnp.float32).astype(jnp.bfloat16)
            mlp_loc = lax.psum_scatter(mlp_part, 'tp', scatter_dimension=1, tiled=True)
            hidden = (after_attn.astype(jnp.float32) + mlp_loc.astype(jnp.float32)).astype(jnp.bfloat16)
            k_list.append(k_new)
            v_list.append(v_new)
        return hidden, jnp.stack(k_list), jnp.stack(v_list)

    return jax.shard_map(device_fn, mesh=mesh, in_specs=(tok_spec, P('dp'), cache_spec, cache_spec, col_spec, col_spec, col_spec, row_spec, col_spec, row_spec, P(), P()), out_specs=(tok_spec, cache_spec, cache_spec), check_vma=False)
```

profile of v0, /device:TPU:81, one launch (start us, length us, event | category | flops | bytes accessed | tf_op | source)
XLA Modules:
  0.0 769.0 jit_solution(13134286106222390897)
XLA Ops:
  16.0 4.9 fusion.157
  20.9 3.1 copy.15
  24.7 6.3 fusion.158
  31.0 5.2 iota_compare_fusion
  42.4 18.8 %all-gather.5.cloned.1.call-done = bf16[3,384,3072]{2,1,0:T(8,128)(2,1)} async-done(((bf16[3,48,3072]{2,1,0:T(8,128)(2,1)}), bf16[3,384,3072]{2,1,0:T(8,128)(2,1)}) %all-gather.5.cloned.1.call-update) | async-done | bytes 7077904 | tf_op jit(solution)/shard_map/all_gather | solution.py:71
  61.2 5.4 convolution_bitcast_fusion.1
  67.3 28.3 %while.4 = (s32[]{:T(128)}, bf16[3,1,3456,128]{3,2,1,0:T(8,128)(2,1)}, s32[3,4]{1,0:T(4,128)S(1)}, bf16[3,1,384,128]{2,3,0,1:T(8,128)(2,1)S(1)}, s32[]{:T(128)}, /*index=5*/s32[4]{0:T(128)S(1)}, s32[]{:T(128)}) while((s32[]{:T(128)}, bf16[3,1,3456,128]{3,2,1,0:T(8,128)(2,1)}, s32[3,4]{1,0:T(4,128)S(1)}, bf16[3,1,384,128]{2,3,0,1:T(8,128)(2,1)S(1)}, ...), condition=%wide.while_cond, body=%wide.while_body.sunk | while | flops 49181 | bytes 884931 | solution.py:34
  68.0 3.2 and_reduce_fusion.8
  77.5 3.2 and_reduce_fusion.8
  86.9 3.2 and_reduce_fusion.8
  95.7 8.2 %fusion.72 = f32[3,1,4,384,128]{3,4,2,0,1:T(8,128)S(1)} fusion(bf16[3072,4,128,1]{0,2,1,3:T(8,128)(2,1)} %bitcast.282, bf16[3,384,3072]{2,1,0:T(8,128)(2,1)} %all-gather.5.cloned.1.call-done), kind=kOutput, calls=%fused_computation.105 | convolution fusion | flops 3623878656 | bytes 12582912 | tf_op jit(solution)/shard_map/bcd,dkgh->bkgch/dot_general | solution.py:72
  104.8 5.0 fusion.106
  109.9 21.7 %while.5 = (s32[]{:T(128)}, bf16[3,1,3456,128]{3,2,1,0:T(8,128)(2,1)S(1)}, s32[3,4]{1,0:T(4,128)S(1)}, bf16[3,1,384,128]{3,2,1,0:T(8,128)(2,1)S(1)}, s32[]{:T(128)}, /*index=5*/s32[4]{0:T(128)S(1)}, s32[]{:T(128)}) while((s32[]{:T(128)}, bf16[3,1,3456,128]{3,2,1,0:T(8,128)(2,1)S(1)}, s32[3,4]{1,0:T(4,128)S(1)}, ...), condition=%wide.while_cond.1, body=%wide.while_body.1.sunk | while | flops 49181 | bytes 491715 | solution.py:34
  134.6 28.0 %fusion = (f32[3,4,384]{2,1,0:T(4,128)S(1)}, f32[3,4,384,3456]{3,2,1,0:T(8,128)}) fusion(pred[3,384,3456]{2,1,0:T(8,128)(4,1)} %iota_compare_fusion, bf16[3,1,3456,128]{3,2,1,0:T(8,128)(2,1)} %get-tuple-element.8, bf16[3,4,384,64]{2,3,1,0:T(8,128)(2,1)} %fusion.116, bf16[3,4,384,32]{2,3,1,0:T(8,128)(2,1)} %get-tuple-element.116, ...), kind=kOutput, calls=%fused_computation.18 | convolution fusion | flops 4128173568 | bytes 71534592 | tf_op jit(solution)/shard_map/bkgch,bksh->bkgcs/dot_general | solution.py:38
  162.6 26.7 %fusion.2 = f32[3,4,384]{2,1,0:T(4,128)S(1)} fusion(f32[3,4,384,3456]{3,2,1,0:T(8,128)} %get-tuple-element.134, f32[3,4,384]{2,1,0:T(4,128)S(1)} %get-tuple-element.133, pred[3,384,3456]{2,1,0:T(8,128)(4,1)} %iota_compare_fusion), kind=kLoop, calls=%fused_computation.20 | loop fusion | flops 63696384 | bytes 67719168 | tf_op jit(solution)/shard_map/reduce_sum | solution.py:42
  189.3 31.4 %bitcast_convert_fusion.1 = bf16[3,384,3072]{2,1,0:T(8,128)(2,1)} fusion(bf16[4,128,3072,1]{2,1,0,3:T(8,128)(2,1)} %bitcast.285, f32[3,4,384,3456]{3,2,1,0:T(8,128)} %get-tuple-element.134, f32[3,4,384]{2,1,0:T(4,128)S(1)} %get-tuple-element.133, pred[3,384,3456]{2,1,0:T(8,128)(4,1)} %iota_compare_fusion, ...), kind=kOutput, calls=%fused_computation.30 | convolution fusion | flops 7769161728 | bytes 80596992 | tf_op jit(solution)/shard_map/bkgch,kghd->bcd/dot_general | solution.py:80
  221.2 41.8 %reduce-scatter.5.cloned.1.call-done = bf16[3,48,3072]{2,1,0:T(8,128)(2,1)} async-done(((bf16[3,384,3072]{2,1,0:T(8,128)(2,1)}), bf16[3,48,3072]{2,1,0:T(8,128)(2,1)}) %reduce-scatter.5.cloned.1.call-update) | async-done | bytes 884752 | tf_op jit(solution)/shard_map/reduce_scatter | solution.py:81
  266.4 41.4 %all-gather.7.cloned.1.call-done = bf16[3,384,3072]{2,1,0:T(8,128)(2,1)} async-done(((bf16[3,48,3072]{2,1,0:T(8,128)(2,1)}), bf16[3,384,3072]{2,1,0:T(8,128)(2,1)}) %all-gather.7.cloned.1.call-update) | async-done | bytes 7077904 | tf_op jit(solution)/shard_map/all_gather | solution.py:84
  307.9 13.4 %multiply_convert_fusion.1 = bf16[3,384,1152]{2,1,0:T(8,128)(2,1)S(1)} fusion(bf16[3,384,3072]{2,1,0:T(8,128)(2,1)} %all-gather.7.cloned.1.call-done, bf16[2,3072,1152]{2,1,0:T(8,128)(2,1)} %param.20), kind=kOutput, calls=%fused_computation.52 | convolution fusion | flops 8157708288 | bytes 16809984 | tf_op jit(solution)/shard_map/bcd,df->bcf/dot_general | solution.py:85
  321.3 14.5 %fusion.28 = bf16[3,384,3072]{2,1,0:T(8,128)(2,1)} fusion(bf16[3,384,1152]{2,1,0:T(8,128)(2,1)S(1)} %multiply_convert_fusion.1, bf16[2,1152,3072]{2,1,0:T(8,128)(2,1)} %param.21), kind=kOutput, calls=%fused_computation.47 | convolution fusion | flops 8157265920 | bytes 16809984 | tf_op jit(solution)/shard_map/bcf,fd->bcd/dot_general | solution.py:87
  335.9 42.6 %reduce-scatter.7.cloned.1.call-done = bf16[3,48,3072]{2,1,0:T(8,128)(2,1)} async-done(((bf16[3,384,3072]{2,1,0:T(8,128)(2,1)}), bf16[3,48,3072]{2,1,0:T(8,128)(2,1)}) %reduce-scatter.7.cloned.1.call-update) | async-done | bytes 884752 | tf_op jit(solution)/shard_map/reduce_scatter | solution.py:88
  382.0 4.8 copy.24
  386.8 36.5 %all-gather.9.cloned.1.call-done = bf16[3,384,3072]{2,1,0:T(8,128)(2,1)} async-done(((bf16[3,48,3072]{2,1,0:T(8,128)(2,1)}), bf16[3,384,3072]{2,1,0:T(8,128)(2,1)}) %all-gather.9.cloned.1.call-update) | async-done | bytes 7077904 | tf_op jit(solution)/shard_map/all_gather | solution.py:71
  423.3 5.4 convolution_bitcast_fusion
  430.7 6.2 fusion.75
  441.5 31.5 %while.7 = (s32[]{:T(128)}, bf16[3,1,3456,128]{3,2,1,0:T(8,128)(2,1)}, s32[3,4]{1,0:T(4,128)S(1)}, bf16[3,1,384,128]{3,2,1,0:T(8,128)(2,1)}, s32[]{:T(128)}, /*index=5*/s32[4]{0:T(128)S(1)}, s32[]{:T(128)}) while((s32[]{:T(128)}, bf16[3,1,3456,128]{3,2,1,0:T(8,128)(2,1)}, s32[3,4]{1,0:T(4,128)S(1)}, bf16[3,1,384,128]{3,2,1,0:T(8,128)(2,1)}, ...), condition=%wide.while_cond.3, body=%wide.while_body.3.sunk | while | flops 49181 | bytes 491715 | solution.py:34
  442.2 3.3 and_reduce_fusion.11
  445.5 3.5 dynamic-slice_select_fusion.11
  452.7 3.3 and_reduce_fusion.11
  456.0 3.5 dynamic-slice_select_fusion.11
  463.2 3.3 and_reduce_fusion.11
  466.5 3.5 dynamic-slice_select_fusion.11
  474.7 39.3 %while.6 = (s32[]{:T(128)}, bf16[3,1,3456,128]{3,2,1,0:T(8,128)(2,1)S(1)}, s32[3,4]{1,0:T(4,128)S(1)}, bf16[3,1,384,128]{2,3,0,1:T(8,128)(2,1)}, s32[]{:T(128)}, /*index=5*/s32[4]{0:T(128)S(1)}, s32[]{:T(128)}) while((s32[]{:T(128)}, bf16[3,1,3456,128]{3,2,1,0:T(8,128)(2,1)S(1)}, s32[3,4]{1,0:T(4,128)S(1)}, bf16[3,1,384,128]{2,3,0,1:T(8,128)(2,1)}, ...), condition=%wide.while_cond.2, body=%wide.while_body.2.sunk | while | flops 49181 | bytes 884931 | solution.py:34
  475.4 3.3 and_reduce_fusion.10
  481.9 3.4 dynamic-slice_select_fusion.10
  488.7 3.3 and_reduce_fusion.10
  495.1 3.4 dynamic-slice_select_fusion.10
  501.7 3.3 and_reduce_fusion.10
  508.2 3.4 dynamic-slice_select_fusion.10
  514.0 28.8 %fusion.1 = (f32[3,4,384]{2,1,0:T(4,128)}, f32[3,4,384,3456]{3,2,1,0:T(8,128)}) fusion(pred[3,384,3456]{2,1,0:T(8,128)(4,1)} %iota_compare_fusion, bf16[3,1,3456,128]{3,2,1,0:T(8,128)(2,1)S(1)} %get-tuple-element.24, bf16[3,4,384,64]{2,3,1,0:T(8,128)(2,1)} %fusion.117, bf16[3,4,384,32]{2,3,1,0:T(8,128)(2,1)} %get-tuple-element.114, ...), kind=kOutput, calls=%fused_computation.19 | convolution fusion | flops 4128173568 | bytes 71534592 | tf_op jit(solution)/shard_map/bkgch,bksh->bkgcs/dot_general | solution.py:38
  542.8 27.1 %fusion.4 = f32[3,4,384]{2,1,0:T(4,128)} fusion(f32[3,4,384,3456]{3,2,1,0:T(8,128)} %get-tuple-element.136, f32[3,4,384]{2,1,0:T(4,128)} %get-tuple-element.135, pred[3,384,3456]{2,1,0:T(8,128)(4,1)} %iota_compare_fusion), kind=kLoop, calls=%fused_computation.22 | loop fusion | flops 63696384 | bytes 67719168 | tf_op jit(solution)/shard_map/reduce_sum | solution.py:42
  570.0 31.5 %bitcast_convert_fusion = bf16[3,384,3072]{2,1,0:T(8,128)(2,1)} fusion(bf16[4,128,3072,1]{2,1,0,3:T(8,128)(2,1)} %bitcast.284, f32[3,4,384,3456]{3,2,1,0:T(8,128)} %get-tuple-element.136, f32[3,4,384]{2,1,0:T(4,128)} %get-tuple-element.135, pred[3,384,3456]{2,1,0:T(8,128)(4,1)} %iota_compare_fusion, bf16[3,1,3456,128]{3,2,1,0:T(8,128)(2,1)S(1)} %copy-done.3, ...), kind=kOutput, calls=%fused_computation.29 | convolution fusion | flops 7769161728 | bytes 80596992 | tf_op jit(solution)/shard_map/bkgch,kghd->bcd/dot_general | solution.py:80
  601.7 42.4 %reduce-scatter.9.cloned.1.call-done = bf16[3,48,3072]{2,1,0:T(8,128)(2,1)} async-done(((bf16[3,384,3072]{2,1,0:T(8,128)(2,1)}), bf16[3,48,3072]{2,1,0:T(8,128)(2,1)}) %reduce-scatter.9.cloned.1.call-update) | async-done | bytes 884752 | tf_op jit(solution)/shard_map/reduce_scatter | solution.py:81
  647.5 41.4 %all-gather.11.cloned.1.call-done = bf16[3,384,3072]{2,1,0:T(8,128)(2,1)} async-done(((bf16[3,48,3072]{2,1,0:T(8,128)(2,1)}), bf16[3,384,3072]{2,1,0:T(8,128)(2,1)}) %all-gather.11.cloned.1.call-update) | async-done | bytes 7077904 | tf_op jit(solution)/shard_map/all_gather | solution.py:84
  688.9 13.4 %multiply_convert_fusion = bf16[3,384,1152]{2,1,0:T(8,128)(2,1)S(1)} fusion(bf16[3,384,3072]{2,1,0:T(8,128)(2,1)} %all-gather.11.cloned.1.call-done, bf16[2,3072,1152]{2,1,0:T(8,128)(2,1)} %param.20), kind=kOutput, calls=%fused_computation.51 | convolution fusion | flops 8157708288 | bytes 16809984 | tf_op jit(solution)/shard_map/bcd,df->bcf/dot_general | solution.py:85
  702.3 14.5 %fusion.31 = bf16[3,384,3072]{2,1,0:T(8,128)(2,1)} fusion(bf16[3,384,1152]{2,1,0:T(8,128)(2,1)S(1)} %multiply_convert_fusion, bf16[2,1152,3072]{2,1,0:T(8,128)(2,1)} %param.21), kind=kOutput, calls=%fused_computation.48 | convolution fusion | flops 8157265920 | bytes 16809984 | tf_op jit(solution)/shard_map/bcf,fd->bcd/dot_general | solution.py:87
  716.8 9.1 %pad_maximum_fusion = (bf16[2,3,1,3456,128]{4,3,2,1,0:T(8,128)(2,1)}, bf16[2,3,1,3456,128]{4,3,2,1,0:T(8,128)(2,1)}) fusion(bf16[1,3,1,3456,128]{4,3,2,1,0:T(8,128)(2,1)} %bitcast.272, bf16[1,3,1,3456,128]{4,3,2,1,0:T(8,128)(2,1)} %bitcast.275, bf16[1,3,1,3456,128]{4,3,2,1,0:T(8,128)(2,1)} %bitcast.273, bf16[1,3,1,3456,128]{4,3,2,1,0:T(8,128)(2,1)} %bitcast.274), kind=kLoop, calls=%fused_computation.49 | loop fusion | flops 5308416 | bytes 21233664 | tf_op jit(solution)/shard_map/stack | solution.py:92
  725.9 33.6 %reduce-scatter.11.cloned.1.call-done = bf16[3,48,3072]{2,1,0:T(8,128)(2,1)} async-done(((bf16[3,384,3072]{2,1,0:T(8,128)(2,1)}), bf16[3,48,3072]{2,1,0:T(8,128)(2,1)}) %reduce-scatter.11.cloned.1.call-update) | async-done | bytes 884752 | tf_op jit(solution)/shard_map/reduce_scatter | solution.py:88
  (162 shorter events, 112.6 us)
Async XLA Ops:
  7.2 8.6 %copy-start.14 = (s32[3]{0:T(128)S(1)}, s32[3]{0:T(128)}, u32[]{:S(2)}) copy-start(s32[3]{0:T(128)} %constant.31.clone.1) | copy-start | bytes 40
  7.2 8.6 %copy-start.13 = (s32[3]{0:T(128)S(1)}, s32[3]{0:T(128)}, u32[]{:S(2)}) copy-start(s32[3]{0:T(128)} %param.13) | copy-start | bytes 40
  7.2 54.0 %all-gather.5.cloned.1.call-start = ((), (), s32[]{:S(2)}) async-start(), calls=%async_computation.4 | async-start | bytes 7962624 | tf_op jit(solution)/shard_map/all_gather | solution.py:71
  15.7 247.3 %reduce-scatter.5.cloned.1.call-start = ((), (), s32[]{:S(2)}) async-start(), calls=%async_computation.5 | async-start | bytes 7962624 | tf_op jit(solution)/shard_map/reduce_scatter | solution.py:81
  24.1 12.1 %slice-start = ((s8[5308416]{0:T(1024)(128)(4,1)}), s8[4194304]{0:T(1024)(128)(4,1)S(1)}, s32[]{:S(2)}) async-start(s8[5308416]{0:T(1024)(128)(4,1)} %bitcast.276), calls=%async_computation.12 | async-start | bytes 8388608
  24.7 11.5 %slice-start.1 = ((s8[5308416]{0:T(1024)(128)(4,1)}), s8[1114112]{0:T(1024)(128)(4,1)S(1)}, s32[]{:S(2)}) async-start(s8[5308416]{0:T(1024)(128)(4,1)} %bitcast.276), calls=%async_computation.13 | async-start | bytes 2228224
  36.2 4.1 slice-start.2
  36.2 4.4 slice-start.3
  42.4 24.9 %copy-start.8 = (s32[4]{0:T(128)S(1)}, s32[4]{0:T(128)}, u32[]{:S(2)}) copy-start(s32[4]{0:T(128)} %constant.258) | copy-start | bytes 52
  95.7 9.2 %copy-start.15 = (bf16[2,3072,128]{2,1,0:T(8,128)(2,1)S(1)}, bf16[2,3072,128]{2,1,0:T(8,128)(2,1)}, u32[]{:S(2)}) copy-start(bf16[2,3072,128]{2,1,0:T(8,128)(2,1)} %param.18) | copy-start | bytes 4718596
  103.9 6.0 copy-start.7
  131.6 57.7 %copy-start.4 = (bf16[3,1,3456,128]{3,2,1,0:T(8,128)(2,1)}, bf16[3,1,3456,128]{3,2,1,0:T(8,128)(2,1)S(1)}, u32[]{:S(2)}) copy-start(bf16[3,1,3456,128]{3,2,1,0:T(8,128)(2,1)S(1)} %get-tuple-element.16) | copy-start | bytes 7962628
  220.7 42.3 %copy-start = (bf16[3,48,3072]{2,1,0:T(8,128)(2,1)S(1)}, bf16[3,48,3072]{2,1,0:T(8,128)(2,1)}, u32[]{:S(2)}) copy-start(bf16[3,48,3072]{2,1,0:T(8,128)(2,1)} %param.12) | copy-start | bytes 2654212
  220.7 87.1 %all-gather.7.cloned.1.call-start = ((), (), s32[]{:S(2)}) async-start(), calls=%async_computation.6 | async-start | bytes 7962624 | tf_op jit(solution)/shard_map/all_gather | solution.py:84
  266.3 112.1 %reduce-scatter.7.cloned.1.call-start = ((), (), s32[]{:S(2)}) async-start(), calls=%async_computation.7 | async-start | bytes 7962624 | tf_op jit(solution)/shard_map/reduce_scatter | solution.py:88
  335.8 44.6 %copy-start.11 = (f32[1,1,3072]{2,1,0:T(1,128)S(1)}, f32[1,1,3072]{2,1,0:T(1,128)}, u32[]{:S(2)}) copy-start(f32[1,1,3072]{2,1,0:T(1,128)} %get-tuple-element.124) | copy-start | bytes 36868
  335.8 44.5 %copy-start.12 = (f32[1,1,3072]{2,1,0:T(1,128)S(1)}, f32[1,1,3072]{2,1,0:T(1,128)}, u32[]{:S(2)}) copy-start(f32[1,1,3072]{2,1,0:T(1,128)} %get-tuple-element.128) | copy-start | bytes 36868
  335.8 87.4 %all-gather.9.cloned.1.call-start = ((), (), s32[]{:S(2)}) async-start(), calls=%async_computation.8 | async-start | bytes 7962624 | tf_op jit(solution)/shard_map/all_gather | solution.py:71
  381.8 262.3 %reduce-scatter.9.cloned.1.call-start = ((), (), s32[]{:S(2)}) async-start(), calls=%async_computation.9 | async-start | bytes 7962624 | tf_op jit(solution)/shard_map/reduce_scatter | solution.py:81
  382.0 41.3 %copy-start.6 = (bf16[2,3072,128]{2,1,0:T(8,128)(2,1)S(1)}, bf16[2,3072,128]{2,1,0:T(8,128)(2,1)}, u32[]{:S(2)}) copy-start(bf16[2,3072,128]{2,1,0:T(8,128)(2,1)} %param.17) | copy-start | bytes 4718596
  423.3 7.4 copy-start.5
  436.8 1.9 copy-start.16
  438.7 36.0 %copy-start.1 = (bf16[3,1,3456,128]{3,2,1,0:T(8,128)(2,1)S(1)}, bf16[3,1,3456,128]{3,2,1,0:T(8,128)(2,1)}, u32[]{:S(2)}) copy-start(bf16[3,1,3456,128]{3,2,1,0:T(8,128)(2,1)} %get-tuple-element.314) | copy-start | bytes 7962628
  514.0 28.8 %copy-start.2 = (bf16[3,1,3456,128]{3,2,1,0:T(8,128)(2,1)}, bf16[3,1,3456,128]{3,2,1,0:T(8,128)(2,1)S(1)}, u32[]{:S(2)}) copy-start(bf16[3,1,3456,128]{3,2,1,0:T(8,128)(2,1)S(1)} %get-tuple-element.24) | copy-start | bytes 7962628
  542.8 27.1 %copy-start.3 = (bf16[3,1,3456,128]{3,2,1,0:T(8,128)(2,1)S(1)}, bf16[3,1,3456,128]{3,2,1,0:T(8,128)(2,1)}, u32[]{:S(2)}) copy-start(bf16[3,1,3456,128]{3,2,1,0:T(8,128)(2,1)} %get-tuple-element.32) | copy-start | bytes 7962628
  601.6 44.4 %copy-start.9 = (f32[1,1,3072]{2,1,0:T(1,128)S(1)}, f32[1,1,3072]{2,1,0:T(1,128)}, u32[]{:S(2)}) copy-start(f32[1,1,3072]{2,1,0:T(1,128)} %get-tuple-element.121) | copy-start | bytes 36868
  601.6 44.4 %copy-start.10 = (f32[1,1,3072]{2,1,0:T(1,128)S(1)}, f32[1,1,3072]{2,1,0:T(1,128)}, u32[]{:S(2)}) copy-start(f32[1,1,3072]{2,1,0:T(1,128)} %get-tuple-element.125) | copy-start | bytes 36868
  601.6 87.3 %all-gather.11.cloned.1.call-start = ((), (), s32[]{:S(2)}) async-start(), calls=%async_computation.10 | async-start | bytes 7962624 | tf_op jit(solution)/shard_map/all_gather | solution.py:84
  647.4 112.1 %reduce-scatter.11.cloned.1.call-start = ((), (), s32[]{:S(2)}) async-start(), calls=%async_computation.11 | async-start | bytes 7962624 | tf_op jit(solution)/shard_map/reduce_scatter | solution.py:88
Sparse Core Ops, SparseCore 0:
  15.8 45.3 all-gather.4
  220.9 42.1 reduce-scatter.4
  266.5 41.3 all-gather.6
  335.9 42.4 reduce-scatter.6
  381.9 41.3 all-gather.8
  601.7 42.3 reduce-scatter.8
  647.5 41.3 all-gather.10
  716.9 42.4 reduce-scatter.10
where the time goes:
time: 781 us; the launch traced here: 769 us
  waiting for transfers between devices  299 us (38%)
  matrix products  208 us (27%)
  other arithmetic  170 us (22%)
  local copies, waits for them, and re-layouts  75.9 us (10%)
  between operations  14.9 us (2%)
    reduce_scatter x2, waiting for transfers between devices, device_fn(): lax.psum_scatter(attn_part, 'tp', scatter_dimension=1, tiled=True)  84.2 us
    all_gather x2, waiting for transfers between devices, device_fn(): normed_mlp_all = lax.all_gather(normed_mlp, 'tp', axis=1, tiled=True)  82.8 us
    reduce_scatter x2, waiting for transfers between devices, device_fn(): mlp_loc = lax.psum_scatter(mlp_part, 'tp', scatter_dimension=1, tiled=True)  76.1 us
    scatter x24, other arithmetic  72.7 us
    dot_general x2, matrix products, device_fn(): jnp.einsum('bkgch,kghd->bcd', context, w_o[layer].reshape(kv_loc, group_s...  62.9 us
    dot_general x2, matrix products, attention(): jnp.einsum('bkgch,bksh->bkgcs', q_rot, k_all, preferred_element_type=jnp....  56.8 us
    all_gather x2, waiting for transfers between devices, device_fn(): normed_all = lax.all_gather(normed, 'tp', axis=1, tiled=True)  55.3 us
    reduce_sum x2, other arithmetic, attention(): row_sum = jnp.sum(weights, axis=-1, keepdims=True)  53.8 us
  transfers between devices with their start and end apart: 8, of which 8 were waited for; matrix products, arithmetic and copies ran while one was open for 5% of the time, Pallas kernels for 0%

commit v1 on v0

v1 whole, which is shorter than its diff:
```python
import functools
import math

import jax
import jax.numpy as jnp
from jax import lax
from jax.experimental import pallas as pl
from jax.experimental.pallas import tpu as pltpu
from jax.sharding import PartitionSpec as P

LN_EPS = 1e-5
ROPE_BASE = 10000.0
NEG_BIG = -1e30
CORES = 2
CHIPS = 4
GSLOTS = 3


def rope_tables(positions, head_dim):
    rot_dim = head_dim // 2
    half_rot = rot_dim // 2
    inv_freq = ROPE_BASE ** (-(jnp.arange(half_rot, dtype=jnp.float32) * (2.0 / rot_dim)))
    angles = positions.astype(jnp.float32)[..., None] * inv_freq
    cos_a = jnp.cos(angles)
    sin_a = jnp.sin(angles)
    ones = jnp.ones(cos_a.shape[:-1] + (head_dim - rot_dim,), jnp.float32)
    zeros_r = jnp.zeros_like(ones)
    zeros_h = jnp.zeros_like(sin_a)
    cos_t = jnp.concatenate([cos_a, cos_a, ones], axis=-1)
    sin_lo = jnp.concatenate([-sin_a, zeros_h, zeros_r], axis=-1)
    sin_hi = jnp.concatenate([zeros_h, sin_a, zeros_r], axis=-1)
    return cos_t, sin_lo, sin_hi


def layers_kernel(dims, start_ref, x_ref, gain_ref, bias_ref, cos_ref, slo_ref, shi_ref, kc_ref, vc_ref,
                  wq_ref, wk_ref, wv_ref, wo_ref, wu_ref, wd_ref,
                  xo_ref, kn_ref, vn_ref,
                  gath, part, pairin, pair, d2in, fin, wqkv, wov, wuv, wdv, kbuf, vbuf, qbuf, cbuf, abuf, sbuf, pbuf,
                  ag_s, ag_r, dd_s, dd_r, d2_s, d2_r, f_s, f_r, w_sem, kv_sem, kn_sem):
    n_layers, n_seq, tok, d_model, heads, head_dim, prefix, ff = dims
    new_len = tok * CORES * CHIPS
    half = d_model // 2
    steps = n_layers * 2 * n_seq
    tp_idx = lax.axis_index('tp')
    chip = tp_idx // CORES
    core = tp_idx % CORES
    sib = 1 - core
    rchip = (chip + 1) % CHIPS
    lchip = (chip + CHIPS - 1) % CHIPS
    ochip = (chip + 2) % CHIPS
    right = {'tp': rchip * CORES + core}
    left = {'tp': lchip * CORES + core}
    sibling = {'tp': chip * CORES + sib}
    lo = pl.ds(0, half)
    hi = pl.ds(half, half)

    def remote(src, dst, s_sem, r_sem, dev):
        return pltpu.make_async_remote_copy(src_ref=src, dst_ref=dst, send_sem=s_sem, recv_sem=r_sem,
                                            device_id=dev, device_id_type=pl.DeviceIdType.MESH)

    def ag_copy(m, k):
        g = m % GSLOTS
        where_from = [(chip, core, lo, right), (chip, core, hi, right), (chip, core, hi, left), (chip, core, lo, left),
                      (chip, core, None, sibling), (lchip, core, lo, right), (rchip, core, hi, left),
                      (lchip, core, None, sibling), (rchip, core, None, sibling), (ochip, core, lo, sibling),
                      (ochip, core, hi, sibling)]
        c, r, cols, dev = where_from[k]
        ref = gath.at[g, c, r] if cols is None else gath.at[g, c, r, :, cols]
        return remote(ref, ref, ag_s.at[g, k], ag_r.at[g, k], dev)

    def ag_start(m, ks):
        for k in ks:
            ag_copy(m, k).start()

    def ag_wait_recv(m, ks):
        for k in ks:
            ag_copy(m, k).wait_recv()

    def dd_copy():
        return remote(part.at[:, sib], pairin, dd_s, dd_r, sibling)

    def d2_copy(n, k):
        p = n % 2
        cols, dev = [(lo, right), (hi, left)][k]
        return remote(pair.at[p, ochip, :, cols], d2in.at[p, k], d2_s.at[p, k], d2_r.at[p, k], dev)

    def f_copy(n, k):
        p = n % 2
        f = n % 3
        c, cols, side, dev = [(rchip, hi, 0, right), (rchip, lo, 0, right), (lchip, lo, 1, left), (lchip, hi, 1, left)][k]
        return remote(pair.at[p, c, :, cols], fin.at[f, side, :, cols], f_s.at[f, k], f_r.at[f, k], dev)

    def attn_weights(l):
        qw = heads * head_dim
        return [pltpu.make_async_copy(wq_ref.at[l], wqkv.at[:, pl.ds(0, qw)], w_sem.at[0]),
                pltpu.make_async_copy(wk_ref.at[l], wqkv.at[:, pl.ds(qw, head_dim)], w_sem.at[1]),
                pltpu.make_async_copy(wv_ref.at[l], wqkv.at[:, pl.ds(qw + head_dim, head_dim)], w_sem.at[2]),
                pltpu.make_async_copy(wo_ref.at[l], wov, w_sem.at[3])]

    def mlp_weights(l):
        return [pltpu.make_async_copy(wu_ref.at[l], wuv, w_sem.at[4]),
                pltpu.make_async_copy(wd_ref.at[l], wdv, w_sem.at[5])]

    def kv_loads(a):
        l, b, p = a // n_seq, a % n_seq, a % 2
        rows = pl.ds(0, prefix)
        return [pltpu.make_async_copy(kc_ref.at[l, b, 0, rows], kbuf.at[p, rows], kv_sem.at[p, 0]),
                pltpu.make_async_copy(vc_ref.at[l, b, 0, rows], vbuf.at[p, rows], kv_sem.at[p, 1])]

    def start(copies):
        for c in copies:
            c.start()

    def wait(copies):
        for c in copies:
            c.wait()

    def norm_into(b, idx, m):
        xf = xo_ref[b].astype(jnp.float32)
        mean = jnp.sum(xf, axis=-1, keepdims=True) * (1.0 / d_model)
        cen = xf - mean
        var = jnp.sum(cen * cen, axis=-1, keepdims=True) * (1.0 / d_model)
        out = cen * lax.rsqrt(var + LN_EPS) * gain_ref[idx] + bias_ref[idx]
        gath[m % GSLOTS, chip, core] = out.astype(jnp.bfloat16)

    def pair_sum(n):
        dd_copy().wait()
        for k in range(11):
            ag_copy(n, k).wait_send()

        @pl.when(n >= 2)
        def _():
            for k in range(2):
                d2_copy(n - 2, k).wait_send()
            for k in range(4):
                f_copy(n - 2, k).wait_send()

        p = n % 2

        def add(c):
            pair[p, c] = (part[c, core].astype(jnp.float32) + pairin[c].astype(jnp.float32)).astype(jnp.bfloat16)

        add(ochip)
        d2_copy(n, 0).start()
        d2_copy(n, 1).start()
        add(rchip)
        f_copy(n, 0).start()
        add(lchip)
        f_copy(n, 2).start()
        add(chip)

    def add_through(n):
        p = n % 2
        d2_copy(n, 0).wait_recv()
        pair[p, rchip, :, lo] = (pair[p, rchip, :, lo].astype(jnp.float32) + d2in[p, 0].astype(jnp.float32)).astype(jnp.bfloat16)
        f_copy(n, 1).start()
        d2_copy(n, 1).wait_recv()
        pair[p, lchip, :, hi] = (pair[p, lchip, :, hi].astype(jnp.float32) + d2in[p, 1].astype(jnp.float32)).astype(jnp.bfloat16)
        f_copy(n, 3).start()

    def finalize(n):
        for k in range(4):
            f_copy(n, k).wait_recv()
        p = n % 2
        f = n % 3
        b = n % n_seq
        o = pair[p, chip].astype(jnp.float32) + fin[f, 0].astype(jnp.float32) + fin[f, 1].astype(jnp.float32)
        o = o.astype(jnp.bfloat16).astype(jnp.float32)
        xo_ref[b] = (xo_ref[b].astype(jnp.float32) + o).astype(jnp.bfloat16)

    def forward(m):
        ag_wait_recv(m, (0,))
        ag_start(m, (5,))
        ag_wait_recv(m, (2,))
        ag_start(m, (6,))
        ag_wait_recv(m, (1,))
        ag_start(m, (7,))
        ag_wait_recv(m, (3,))
        ag_start(m, (8,))

    def forward_far(m):
        ag_wait_recv(m, (5,))
        ag_start(m, (9,))
        ag_wait_recv(m, (6,))
        ag_start(m, (10,))

    def gathered(n):
        ag_wait_recv(n, (4, 7, 8, 9, 10))

    def event_add(n):
        @pl.when(n >= 1)
        def _():
            add_through(n - 1)

    def event_forward(n):
        @pl.when(n + 1 < steps)
        def _():
            forward(n + 1)

    def after_compute(n):
        dd_copy().start()
        pair_sum(n)

        @pl.when(n >= 1)
        def _():
            finalize(n - 1)

            @pl.when(n + 2 < steps)
            def _():
                norm_into((n + 2) % n_seq, (n + 2) // n_seq, n + 2)
                ag_start(n + 2, range(5))

        @pl.when(n + 1 < steps)
        def _():
            forward_far(n + 1)

    def rows_of(g):
        return gath[g].reshape(new_len, d_model)

    def put_part(cols, val):
        part[:, :, :, cols] = val.astype(jnp.bfloat16).reshape(CHIPS, CORES, tok, val.shape[-1])

    NT = (((1,), (1,)), ((), ()))
    tile = 256

    def attn_step(l, b, n):
        a = l * n_seq + b
        p = a % 2
        wait(kv_loads(a))

        @pl.when(a + 1 < n_layers * n_seq)
        def _():
            start(kv_loads(a + 1))

        gathered(n)
        g = n % GSLOTS
        cos_t, sin_lo, sin_hi = cos_ref[b], slo_ref[b], shi_ref[b]
        quarter = head_dim // 4

        def rotate(val):
            return (val * cos_t + pltpu.roll(val, head_dim - quarter, 1) * sin_lo + pltpu.roll(val, quarter, 1) * sin_hi).astype(jnp.bfloat16)

        kv = jnp.dot(rows_of(g), wqkv[:, pl.ds(heads * head_dim, 2 * head_dim)], preferred_element_type=jnp.float32)
        kbuf[p, pl.ds(prefix, new_len)] = rotate(kv[:, :head_dim])
        vbuf[p, pl.ds(prefix, new_len)] = kv[:, head_dim:].astype(jnp.bfloat16)
        outs = [pltpu.make_async_copy(kbuf.at[p, pl.ds(prefix, new_len)], kn_ref.at[l, b], kn_sem.at[0]),
                pltpu.make_async_copy(vbuf.at[p, pl.ds(prefix, new_len)], vn_ref.at[l, b], kn_sem.at[1])]
        start(outs)

        @pl.loop(0, heads // 2)
        def _(j):
            q2 = jnp.dot(rows_of(g), wqkv[:, pl.ds(pl.multiple_of(j * tile, tile), tile)], preferred_element_type=jnp.float32)
            qbuf[2 * j] = rotate(q2[:, :head_dim])
            qbuf[2 * j + 1] = rotate(q2[:, head_dim:])

        event_add(n)
        first_len = start_ref[b]
        chunk = math.gcd(prefix, 512)
        chunks = [(c, chunk) for c in range(0, prefix, chunk)] + [(prefix, new_len)]
        c_exp = head_dim ** -0.5 * math.log2(math.e)
        neg = NEG_BIG * head_dim ** 0.5

        @pl.loop(0, heads)
        def _(h):
            q = qbuf[h]
            peak = None
            for c0, cl in chunks:
                s = lax.dot_general(q, kbuf[p, pl.ds(c0, cl)], NT, preferred_element_type=jnp.float32)
                col = lax.broadcasted_iota(jnp.int32, (new_len, cl), 1)
                if c0 >= prefix:
                    s = jnp.where(col <= lax.broadcasted_iota(jnp.int32, (new_len, cl), 0), s, neg)
                else:
                    s = jnp.where(col < first_len - c0, s, neg)
                sbuf[:, pl.ds(c0, cl)] = s
                for k in range(0, cl, 128):
                    piece = s[:, k:k + 128]
                    peak = piece if peak is None else jnp.maximum(peak, piece)
            peak = jnp.max(peak, axis=-1, keepdims=True)
            total = None
            for c0, cl in chunks:
                e = jnp.exp2((sbuf[:, pl.ds(c0, cl)] - peak) * c_exp)
                pbuf[:, pl.ds(c0, cl)] = e.astype(jnp.bfloat16)
                for k in range(0, cl, 128):
                    piece = e[:, k:k + 128]
                    total = piece if total is None else total + piece
            total = jnp.sum(total, axis=-1, keepdims=True)
            ctx = jnp.dot(pbuf[...], vbuf[p], preferred_element_type=jnp.float32) / total
            cbuf[:, pl.ds(pl.multiple_of(h * head_dim, head_dim), head_dim)] = ctx.astype(jnp.bfloat16)

            @pl.when(h == 1)
            def _():
                event_forward(n)

        @pl.loop(0, d_model // tile)
        def _(j):
            cols = pl.ds(pl.multiple_of(j * tile, tile), tile)
            put_part(cols, jnp.dot(cbuf[...], wov[:, cols], preferred_element_type=jnp.float32))

        wait(outs)
        after_compute(n)

    def mlp_step(n):
        gathered(n)
        g = n % GSLOTS

        def up(cols):
            val = jnp.dot(rows_of(g), wuv[:, cols], preferred_element_type=jnp.float32)
            val = jnp.maximum(val, 0.0)
            abuf[:, cols] = (val * val).astype(jnp.bfloat16)

        @pl.loop(0, ff // tile)
        def _(j):
            up(pl.ds(pl.multiple_of(j * tile, tile), tile))

        if ff % tile:
            up(pl.ds(ff - ff % tile, ff % tile))
        event_add(n)
        n_tiles = d_model // tile

        @pl.loop(0, n_tiles)
        def _(j):
            cols = pl.ds(pl.multiple_of(j * tile, tile), tile)
            put_part(cols, jnp.dot(abuf[...], wdv[:, cols], preferred_element_type=jnp.float32))

            @pl.when(j == n_tiles // 2)
            def _():
                event_forward(n)

        after_compute(n)

    start(attn_weights(0))
    start(kv_loads(0))
    start(mlp_weights(0))
    xo_ref[...] = x_ref[...]

    barrier = pltpu.get_barrier_semaphore()
    for dev in (left, right, sibling):
        pl.semaphore_signal(barrier, inc=1, device_id=dev, device_id_type=pl.DeviceIdType.MESH)
    pl.semaphore_wait(barrier, 3)
    for b in range(n_seq):
        norm_into(b, 0, b)
        ag_start(b, range(5))
    forward(0)
    forward_far(0)

    @pl.loop(0, n_layers)
    def _(l):
        @pl.when(l >= 1)
        def _():
            start(mlp_weights(l))

        wait(attn_weights(l))

        @pl.loop(0, n_seq)
        def _(b):
            attn_step(l, b, l * 2 * n_seq + b)

        @pl.when(l + 1 < n_layers)
        def _():
            start(attn_weights(l + 1))

        wait(mlp_weights(l))

        @pl.loop(0, n_seq)
        def _(b):
            mlp_step(l * 2 * n_seq + n_seq + b)

    add_through(steps - 1)
    finalize(steps - 1)
    for n in (steps - 2, steps - 1):
        for k in range(2):
            d2_copy(n, k).wait_send()
        for k in range(4):
            f_copy(n, k).wait_send()


def run_layers(start_pos, x_loc, k_cache, v_cache, w_q, w_k, w_v, w_o, w_up, w_down, ln_gain, ln_bias, new_len):
    n_layers, n_seq, _, cache_len, head_dim = k_cache.shape
    tok, d_model = x_loc.shape[1:]
    heads = w_q.shape[2] // head_dim
    prefix = cache_len - new_len
    ff = w_up.shape[2]
    bf, f32 = jnp.bfloat16, jnp.float32
    positions = start_pos[:, None] + jnp.arange(new_len, dtype=jnp.int32)[None, :]
    cos_t, sin_lo, sin_hi = rope_tables(positions, head_dim)
    gain = (1.0 + ln_gain.astype(f32)).reshape(n_layers * 2, 1, d_model)
    bias = ln_bias.astype(f32).reshape(n_layers * 2, 1, d_model)
    vm = pl.BlockSpec(memory_space=pltpu.VMEM)
    hb = pl.BlockSpec(memory_space=pl.ANY)
    dims = (n_layers, n_seq, tok, d_model, heads, head_dim, prefix, ff)
    dma = pltpu.SemaphoreType.DMA
    return pl.pallas_call(
        functools.partial(layers_kernel, dims),
        out_shape=(jax.ShapeDtypeStruct(x_loc.shape, bf),
                   jax.ShapeDtypeStruct((n_layers, n_seq, new_len, head_dim), bf),
                   jax.ShapeDtypeStruct((n_layers, n_seq, new_len, head_dim), bf)),
        in_specs=[pl.BlockSpec(memory_space=pltpu.SMEM)] + [vm] * 6 + [hb] * 8,
        out_specs=(vm, hb, hb),
        scratch_shapes=[
            pltpu.VMEM((GSLOTS, CHIPS, CORES, tok, d_model), bf),
            pltpu.VMEM((CHIPS, CORES, tok, d_model), bf),
            pltpu.VMEM((CHIPS, tok, d_model), bf),
            pltpu.VMEM((2, CHIPS, tok, d_model), bf),
            pltpu.VMEM((2, 2, tok, d_model // 2), bf),
            pltpu.VMEM((3, 2, tok, d_model), bf),
            pltpu.VMEM((d_model, (heads + 2) * head_dim), bf),
            pltpu.VMEM((heads * head_dim, d_model), bf),
            pltpu.VMEM((d_model, ff), bf),
            pltpu.VMEM((ff, d_model), bf),
            pltpu.VMEM((2, cache_len, head_dim), bf),
            pltpu.VMEM((2, cache_len, head_dim), bf),
            pltpu.VMEM((heads, new_len, head_dim), bf),
            pltpu.VMEM((new_len, heads * head_dim), bf),
            pltpu.VMEM((new_len, ff), bf),
            pltpu.VMEM((new_len, cache_len), f32),
            pltpu.VMEM((new_len, cache_len), bf),
            dma((GSLOTS, 11)), dma((GSLOTS, 11)), dma, dma, dma((2, 2)), dma((2, 2)), dma((3, 4)), dma((3, 4)),
            dma((6,)), dma((2, 2)), dma((2,)),
        ],
        compiler_params=pltpu.CompilerParams(collective_id=0, has_side_effects=True, vmem_limit_bytes=67043328),
        name='layers',
    )(start_pos, x_loc, gain, bias, cos_t, sin_lo, sin_hi, k_cache, v_cache, w_q, w_k, w_v, w_o, w_up, w_down)


def merge_kernel(new_len, cache_len, n_seq, start_ref, kc_ref, vc_ref, kn_ref, vn_ref, ko_ref, vo_ref):
    first = start_ref[lax.rem(pl.program_id(0), n_seq)]
    span = new_len + 16
    base = pl.multiple_of(jnp.minimum(first // 16 * 16, cache_len - span), 16)
    shift = first - base
    row = lax.broadcasted_iota(jnp.int32, (span, kc_ref.shape[-1]), 0)
    inside = jnp.logical_and(row >= shift, row < shift + new_len)
    for old, new, out in ((kc_ref, kn_ref, ko_ref), (vc_ref, vn_ref, vo_ref)):
        out[...] = old[...]
        fresh = new[0].astype(jnp.float32)
        fresh = jnp.concatenate([fresh, jnp.zeros((16, fresh.shape[-1]), jnp.float32)], axis=0)
        fresh = pltpu.roll(fresh, shift, 0)
        kept = old[0, pl.ds(base, span), :].astype(jnp.float32)
        out[0, pl.ds(base, span), :] = jnp.where(inside, fresh, kept).astype(jnp.bfloat16)


def merge_caches(start_pos, k_cache, v_cache, k_new, v_new):
    n_layers, n_seq, kv, cache_len, head_dim = k_cache.shape
    new_len = k_new.shape[2]
    blocks = n_layers * n_seq
    flat = lambda c: c.reshape(blocks, cache_len, head_dim)
    whole = pl.BlockSpec((1, cache_len, head_dim), lambda i, s: (i, 0, 0))
    fresh = pl.BlockSpec((1, new_len, head_dim), lambda i, s: (i, 0, 0))
    shape = jax.ShapeDtypeStruct((blocks, cache_len, head_dim), jnp.bfloat16)
    k_out, v_out = pl.pallas_call(
        functools.partial(merge_kernel, new_len, cache_len, n_seq),
        out_shape=(shape, shape),
        grid_spec=pltpu.PrefetchScalarGridSpec(num_scalar_prefetch=1, grid=(blocks,), in_specs=[whole, whole, fresh, fresh], out_specs=[whole, whole]),
        name='merge',
    )(start_pos, flat(k_cache), flat(v_cache), k_new.reshape(blocks, new_len, head_dim), v_new.reshape(blocks, new_len, head_dim))
    return k_out.reshape(k_cache.shape), v_out.reshape(v_cache.shape)


def solution(mesh):
    tp_size = mesh.shape['tp']
    assert tp_size == CORES * CHIPS
    tok_spec = P('dp', 'tp', None)
    cache_spec = P(None, 'dp', 'tp', None, None)
    col_spec = P(None, None, 'tp')
    row_spec = P(None, 'tp', None)

    def device_fn(x_loc, start_pos, k_cache, v_cache, w_q, w_k, w_v, w_o, w_up, w_down, ln_gain, ln_bias):
        hidden, k_new, v_new = run_layers(start_pos, x_loc, k_cache, v_cache, w_q, w_k, w_v, w_o, w_up, w_down, ln_gain, ln_bias, x_loc.shape[1] * tp_size)
        k_out, v_out = merge_caches(start_pos, k_cache, v_cache, k_new, v_new)
        return hidden, k_out, v_out

    return jax.shard_map(device_fn, mesh=mesh, in_specs=(tok_spec, P('dp'), cache_spec, cache_spec, col_spec, col_spec, col_spec, row_spec, col_spec, row_spec, P(), P()), out_specs=(tok_spec, cache_spec, cache_spec), check_vma=False)
```

time: 781 us -> 352 us (0.45); the launches traced: 769 us -> 351 us
  Pallas kernels: 0 us -> 342 us
  waiting for transfers between devices: 299 us -> 0 us
  matrix products: 208 us -> 0 us
  other arithmetic: 170 us -> 5.33 us
  local copies, waits for them, and re-layouts: 75.9 us -> 3.2 us
  between operations: 14.9 us -> 0.68 us
    pallas_call x0 -> x2, Pallas kernels: none -> 342 us  [the longest x1 332 us: run_layers(): pl.pallas_call(functools.partial(layers_kernel, dims), out_shape=(jax.Sha...]
    dot_general x14 -> x0, matrix products: 208 us -> none  [the longest x2 62.9 us: device_fn(): jnp.einsum('bkgch,kghd->bcd', context, w_o[layer].reshape(kv_loc, group_s...]
    reduce_scatter x4 -> x0, waiting for transfers between devices: 160 us -> none  [the longest x2 84.2 us: device_fn(): lax.psum_scatter(attn_part, 'tp', scatter_dimension=1, tiled=True)]
    all_gather x4 -> x0, waiting for transfers between devices: 138 us -> none  [the longest x2 82.8 us: device_fn(): normed_mlp_all = lax.all_gather(normed_mlp, 'tp', axis=1, tiled=True)]
    scatter x25 -> x0, other arithmetic: 72.7 us -> none
    reduce_sum x10 -> x0, other arithmetic: 62.4 us -> none  [the longest x2 53.8 us: attention(): row_sum = jnp.sum(weights, axis=-1, keepdims=True)]
    scatter x48 -> x0, local copies, waits for them, and re-layouts: 47.9 us -> none
    slice x6 -> x0, local copies, waits for them, and re-layouts: 19.8 us -> none  [the longest x3 12.8 us: device_fn(): w_q[layer].reshape(d_model, kv_loc, group_size, head_dim)]
  transfers between devices with their start and end apart: 8 -> 0, of which waited for: 8 -> 0; matrix products, arithmetic and copies ran while one was open for 5% -> 0% of each run, Pallas kernels for 0% -> 0%
where the time goes in v1:
time: 352 us; the launch traced here: 351 us
  Pallas kernels  342 us (97%)
  other arithmetic  5.33 us (2%)
    pallas_call x1, Pallas kernels, run_layers(): pl.pallas_call(functools.partial(layers_kernel, dims), out_shape=(jax.Sha...  332 us
    pallas_call x1, Pallas kernels, merge_caches(): pl.pallas_call(functools.partial(merge_kernel, new_len, cache_len, n_seq)...  10.5 us

profile of v1, /device:TPU:81, one launch (start us, length us, event | category | flops | bytes accessed | tf_op | source)
XLA Modules:
  0.0 351.4 jit_solution(15868379963089816759)
XLA Ops:
  0.6 0.1 pad.8.clone
  0.7 0.1 pad.5.clone
  0.8 0.7 add_convert_fusion
  1.5 0.8 convert_add_fusion
  2.3 0.7 reshape.60.gain_ref
  3.0 1.4 reshape.70.bias_ref
  4.4 2.1 multiply_sine_fusion
  6.6 1.7 maximum_maximum_fusion.2
  8.3 331.7 %layers.1 = (bf16[3,48,3072]{2,1,0:T(8,128)(2,1)}, bf16[2,3,384,128]{3,2,1,0:T(8,128)(2,1)}, bf16[2,3,384,128]{3,2,1,0:T(8,128)(2,1)}) custom-call(s32[3]{0:T(128)} %start_ref.3, bf16[3,48,3072]{2,1,0:T(8,128)(2,1)} %x_ref.1, f32[4,1,3072]{2,1,0:T(1,128)} %reshape.60.gain_ref, f32[4,1,3072]{2,1,0:T(1,128)} %reshape.70.bias_ref, ...), custom_call_target="tpu_custom_call" | custom-call | tf_op jit(solution)/shard_map/layers/pallas_call | solution.py:392
  340.0 0.0 copy-start
  340.0 10.5 %merge.1 = (bf16[6,3456,128]{2,1,0:T(8,128)(2,1)}, bf16[6,3456,128]{2,1,0:T(8,128)(2,1)}) custom-call(s32[3]{0:T(128)} %start_ref.3, bf16[6,3456,128]{2,1,0:T(8,128)(2,1)} %bitcast.10, bf16[6,3456,128]{2,1,0:T(8,128)(2,1)} %bitcast.11, bf16[6,384,128]{2,1,0:T(8,128)(2,1)} %bitcast.12, bf16[6,384,128]{2,1,0:T(8,128)(2,1)} %bitcast.13), custom_call_target="tpu_custom_call" | custom-call | tf_op jit(solution)/shard_map/merge/pallas_call | solution.py:449
  350.5 0.0 copy-done
  350.5 0.9 copy.18
  (4 shorter events, 0.1 us)
Async XLA Ops:
  340.0 10.5 %copy-start = (bf16[3,48,3072]{2,1,0:T(8,128)(2,1)S(1)}, bf16[3,48,3072]{2,1,0:T(8,128)(2,1)}, u32[]{:S(2)}) copy-start(bf16[3,48,3072]{2,1,0:T(8,128)(2,1)} %get-tuple-element.25) | copy-start | bytes 2654212

commit v2 on v1

--- a/solution.py
+++ b/solution.py
@@ -16,26 +16,18 @@
 GSLOTS = 3
 
 
-def rope_tables(positions, head_dim):
+def rope_freqs(head_dim):
     rot_dim = head_dim // 2
     half_rot = rot_dim // 2
     inv_freq = ROPE_BASE ** (-(jnp.arange(half_rot, dtype=jnp.float32) * (2.0 / rot_dim)))
-    angles = positions.astype(jnp.float32)[..., None] * inv_freq
-    cos_a = jnp.cos(angles)
-    sin_a = jnp.sin(angles)
-    ones = jnp.ones(cos_a.shape[:-1] + (head_dim - rot_dim,), jnp.float32)
-    zeros_r = jnp.zeros_like(ones)
-    zeros_h = jnp.zeros_like(sin_a)
-    cos_t = jnp.concatenate([cos_a, cos_a, ones], axis=-1)
-    sin_lo = jnp.concatenate([-sin_a, zeros_h, zeros_r], axis=-1)
-    sin_hi = jnp.concatenate([zeros_h, sin_a, zeros_r], axis=-1)
-    return cos_t, sin_lo, sin_hi
-
-
-def layers_kernel(dims, start_ref, x_ref, gain_ref, bias_ref, cos_ref, slo_ref, shi_ref, kc_ref, vc_ref,
+    return jnp.tile(inv_freq, head_dim // half_rot)[None]
+
+
+def layers_kernel(dims, start_ref, x_ref, lng_ref, lnb_ref, freq_ref, kc_ref, vc_ref,
                   wq_ref, wk_ref, wv_ref, wo_ref, wu_ref, wd_ref,
                   xo_ref, kn_ref, vn_ref,
-                  gath, part, pairin, pair, d2in, fin, wqkv, wov, wuv, wdv, kbuf, vbuf, qbuf, cbuf, abuf, sbuf, pbuf,
+                  gath, part, pairin, pair, d2in, fin, wqkv, wov, wuv, wdv, kbuf, vbuf, qbuf, cbuf, abuf, sbuf_a, sbuf_b,
+                  gain_ref, bias_ref, cos_ref, slo_ref, shi_ref,
                   ag_s, ag_r, dd_s, dd_r, d2_s, d2_r, f_s, f_r, w_sem, kv_sem, kn_sem):
     n_layers, n_seq, tok, d_model, heads, head_dim, prefix, ff = dims
     new_len = tok * CORES * CHIPS
@@ -76,8 +68,9 @@
         for k in ks:
             ag_copy(m, k).wait_recv()
 
-    def dd_copy():
-        return remote(part.at[:, sib], pairin, dd_s, dd_r, sibling)
+    def dd_copy(k):
+        cols = (lo, hi)[k]
+        return remote(part.at[:, sib, :, cols], pairin.at[:, :, cols], dd_s.at[k], dd_r.at[k], sibling)
 
     def d2_copy(n, k):
         p = n % 2
@@ -124,7 +117,6 @@
         gath[m % GSLOTS, chip, core] = out.astype(jnp.bfloat16)
 
     def pair_sum(n):
-        dd_copy().wait()
         for k in range(11):
             ag_copy(n, k).wait_send()
 
@@ -137,17 +129,17 @@
 
         p = n % 2
 
-        def add(c):
-            pair[p, c] = (part[c, core].astype(jnp.float32) + pairin[c].astype(jnp.float32)).astype(jnp.bfloat16)
-
-        add(ochip)
-        d2_copy(n, 0).start()
-        d2_copy(n, 1).start()
-        add(rchip)
-        f_copy(n, 0).start()
-        add(lchip)
-        f_copy(n, 2).start()
-        add(chip)
+        def add(c, cols):
+            pair[p, c, :, cols] = (part[c, core, :, cols].astype(jnp.float32) + pairin[c, :, cols].astype(jnp.float32)).astype(jnp.bfloat16)
+
+        for k, (cols, near, ready, far) in enumerate(((lo, lchip, 2, rchip), (hi, rchip, 0, lchip))):
+            dd_copy(k).wait()
+            add(ochip, cols)
+            d2_copy(n, k).start()
+            add(near, cols)
+            f_copy(n, ready).start()
+            add(far, cols)
+            add(chip, cols)
 
     def add_through(n):
         p = n % 2
@@ -198,7 +190,6 @@
             forward(n + 1)
 
     def after_compute(n):
-        dd_copy().start()
         pair_sum(n)
 
         @pl.when(n >= 1)
@@ -222,6 +213,15 @@
 
     NT = (((1,), (1,)), ((), ()))
     tile = 256
+
+    def product_into_part(lhs, weights):
+        for k in range(2):
+            @pl.loop(0, half // tile)
+            def _(j):
+                cols = pl.ds(pl.multiple_of(k * half + j * tile, tile), tile)
+                put_part(cols, jnp.dot(lhs[...], weights[:, cols], preferred_element_type=jnp.float32))
+
+            dd_copy(k).start()
 
     def attn_step(l, b, n):
         a = l * n_seq + b
@@ -255,47 +255,50 @@
 
         event_add(n)
         first_len = start_ref[b]
-        chunk = math.gcd(prefix, 512)
+        chunk = prefix // 4
         chunks = [(c, chunk) for c in range(0, prefix, chunk)] + [(prefix, new_len)]
         c_exp = head_dim ** -0.5 * math.log2(math.e)
         neg = NEG_BIG * head_dim ** 0.5
-
-        @pl.loop(0, heads)
-        def _(h):
-            q = qbuf[h]
-            peak = None
+        bufs = (sbuf_a, sbuf_b)
+
+        def fold(old, val, op):
+            for k in range(0, val.shape[-1], 128):
+                piece = val[:, k:k + 128]
+                old = piece if old is None else op(old, piece)
+            return old
+
+        def score_chunk(h, q, peak, c0, cl):
+            s = lax.dot_general(q, kbuf[p, pl.ds(c0, cl)], NT, preferred_element_type=jnp.float32)
+            if c0:
+                col = lax.broadcasted_iota(jnp.int32, (new_len, cl), 1)
+                last = lax.broadcasted_iota(jnp.int32, (new_len, cl), 0) if c0 >= prefix else first_len - c0 - 1
+                s = jnp.where(col <= last, s, neg)
+            bufs[h % 2][:, pl.ds(c0, cl)] = s
+            return fold(peak, s, jnp.maximum)
+
+        def weigh_chunk(h, peak, total, acc, c0, cl):
+            e = jnp.exp2((bufs[h % 2][:, pl.ds(c0, cl)] - peak) * c_exp)
+            part_ctx = jnp.dot(e.astype(jnp.bfloat16), vbuf[p, pl.ds(c0, cl)], preferred_element_type=jnp.float32)
+            return fold(total, e, jnp.add), part_ctx if acc is None else acc + part_ctx
+
+        peaks = None
+        for h in range(heads + 1):
+            if h == heads:
+                event_forward(n)
+            q = qbuf[h] if h < heads else None
+            next_peak = total = acc = None
             for c0, cl in chunks:
-                s = lax.dot_general(q, kbuf[p, pl.ds(c0, cl)], NT, preferred_element_type=jnp.float32)
-                col = lax.broadcasted_iota(jnp.int32, (new_len, cl), 1)
-                if c0 >= prefix:
-                    s = jnp.where(col <= lax.broadcasted_iota(jnp.int32, (new_len, cl), 0), s, neg)
-                else:
-                    s = jnp.where(col < first_len - c0, s, neg)
-                sbuf[:, pl.ds(c0, cl)] = s
-                for k in range(0, cl, 128):
-                    piece = s[:, k:k + 128]
-                    peak = piece if peak is None else jnp.maximum(peak, piece)
-            peak = jnp.max(peak, axis=-1, keepdims=True)
-            total = None
-            for c0, cl in chunks:
-                e = jnp.exp2((sbuf[:, pl.ds(c0, cl)] - peak) * c_exp)
-                pbuf[:, pl.ds(c0, cl)] = e.astype(jnp.bfloat16)
-                for k in range(0, cl, 128):
-                    piece = e[:, k:k + 128]
-                    total = piece if total is None else total + piece
-            total = jnp.sum(total, axis=-1, keepdims=True)
-            ctx = jnp.dot(pbuf[...], vbuf[p], preferred_element_type=jnp.float32) / total
-            cbuf[:, pl.ds(pl.multiple_of(h * head_dim, head_dim), head_dim)] = ctx.astype(jnp.bfloat16)
-
-            @pl.when(h == 1)
-            def _():
-                event_forward(n)
-
-        @pl.loop(0, d_model // tile)
-        def _(j):
-            cols = pl.ds(pl.multiple_of(j * tile, tile), tile)
-            put_part(cols, jnp.dot(cbuf[...], wov[:, cols], preferred_element_type=jnp.float32))
-
+                if h < heads:
+                    next_peak = score_chunk(h, q, next_peak, c0, cl)
+                if h:
+                    total, acc = weigh_chunk(h - 1, peaks, total, acc, c0, cl)
+            if h:
+                ctx = acc / jnp.sum(total, axis=-1, keepdims=True)
+                cbuf[:, pl.ds((h - 1) * head_dim, head_dim)] = ctx.astype(jnp.bfloat16)
+            if h < heads:
+                peaks = jnp.max(next_peak, axis=-1, keepdims=True)
+
+        product_into_part(cbuf, wov)
         wait(outs)
         after_compute(n)
 
@@ -315,23 +318,17 @@
         if ff % tile:
             up(pl.ds(ff - ff % tile, ff % tile))
         event_add(n)
-        n_tiles = d_model // tile
-
-        @pl.loop(0, n_tiles)
-        def _(j):
-            cols = pl.ds(pl.multiple_of(j * tile, tile), tile)
-            put_part(cols, jnp.dot(abuf[...], wdv[:, cols], preferred_element_type=jnp.float32))
-
-            @pl.when(j == n_tiles // 2)
-            def _():
-                event_forward(n)
-
+        product_into_part(abuf, wdv)
+        event_forward(n)
         after_compute(n)
 
     start(attn_weights(0))
     start(kv_loads(0))
-    start(mlp_weights(0))
     xo_ref[...] = x_ref[...]
+    for l in range(n_layers):
+        for k in range(2):
+            gain_ref[2 * l + k] = 1.0 + lng_ref[l, k:k + 1].astype(jnp.float32)
+            bias_ref[2 * l + k] = lnb_ref[l, k:k + 1].astype(jnp.float32)
 
     barrier = pltpu.get_barrier_semaphore()
     for dev in (left, right, sibling):
@@ -340,16 +337,25 @@
     for b in range(n_seq):
         norm_into(b, 0, b)
         ag_start(b, range(5))
+    lane = lax.broadcasted_iota(jnp.int32, (new_len, head_dim), 1)
+    row = lax.broadcasted_iota(jnp.int32, (new_len, head_dim), 0)
+    rot = head_dim // 2
+
+    @pl.loop(0, n_seq)
+    def _(b):
+        angle = (start_ref[b] + row).astype(jnp.float32) * freq_ref[...]
+        sin_a = jnp.sin(angle)
+        cos_ref[b] = jnp.where(lane < rot, jnp.cos(angle), 1.0)
+        slo_ref[b] = jnp.where(lane < rot // 2, -sin_a, 0.0)
+        shi_ref[b] = jnp.where(jnp.logical_and(lane >= rot // 2, lane < rot), sin_a, 0.0)
+
     forward(0)
     forward_far(0)
 
     @pl.loop(0, n_layers)
     def _(l):
-        @pl.when(l >= 1)
-        def _():
-            start(mlp_weights(l))
-
         wait(attn_weights(l))
+        start(mlp_weights(l))
 
         @pl.loop(0, n_seq)
         def _(b):
@@ -381,10 +387,6 @@
     prefix = cache_len - new_len
     ff = w_up.shape[2]
     bf, f32 = jnp.bfloat16, jnp.float32
-    positions = start_pos[:, None] + jnp.arange(new_len, dtype=jnp.int32)[None, :]
-    cos_t, sin_lo, sin_hi = rope_tables(positions, head_dim)
-    gain = (1.0 + ln_gain.astype(f32)).reshape(n_layers * 2, 1, d_model)
-    bias = ln_bias.astype(f32).reshape(n_layers * 2, 1, d_model)
     vm = pl.BlockSpec(memory_space=pltpu.VMEM)
     hb = pl.BlockSpec(memory_space=pl.ANY)
     dims = (n_layers, n_seq, tok, d_model, heads, head_dim, prefix, ff)
@@ -394,7 +396,7 @@
         out_shape=(jax.ShapeDtypeStruct(x_loc.shape, bf),
                    jax.ShapeDtypeStruct((n_layers, n_seq, new_len, head_dim), bf),
                    jax.ShapeDtypeStruct((n_layers, n_seq, new_len, head_dim), bf)),
-        in_specs=[pl.BlockSpec(memory_space=pltpu.SMEM)] + [vm] * 6 + [hb] * 8,
+        in_specs=[pl.BlockSpec(memory_space=pltpu.SMEM)] + [vm] * 4 + [hb] * 8,
         out_specs=(vm, hb, hb),
         scratch_shapes=[
             pltpu.VMEM((GSLOTS, CHIPS, CORES, tok, d_model), bf),
@@ -413,46 +415,91 @@
             pltpu.VMEM((new_len, heads * head_dim), bf),
             pltpu.VMEM((new_len, ff), bf),
             pltpu.VMEM((new_len, cache_len), f32),
-            pltpu.VMEM((new_len, cache_len), bf),
-            dma((GSLOTS, 11)), dma((GSLOTS, 11)), dma, dma, dma((2, 2)), dma((2, 2)), dma((3, 4)), dma((3, 4)),
+            pltpu.VMEM((new_len, cache_len), f32),
+            pltpu.VMEM((n_layers * 2, 1, d_model), f32),
+            pltpu.VMEM((n_layers * 2, 1, d_model), f32),
+            pltpu.VMEM((n_seq, new_len, head_dim), f32),
+            pltpu.VMEM((n_seq, new_len, head_dim), f32),
+            pltpu.VMEM((n_seq, new_len, head_dim), f32),
+            dma((GSLOTS, 11)), dma((GSLOTS, 11)), dma((2,)), dma((2,)), dma((2, 2)), dma((2, 2)), dma((3, 4)), dma((3, 4)),
             dma((6,)), dma((2, 2)), dma((2,)),
         ],
         compiler_params=pltpu.CompilerParams(collective_id=0, has_side_effects=True, vmem_limit_bytes=67043328),
         name='layers',
-    )(start_pos, x_loc, gain, bias, cos_t, sin_lo, sin_hi, k_cache, v_cache, w_q, w_k, w_v, w_o, w_up, w_down)
-
-
-def merge_kernel(new_len, cache_len, n_seq, start_ref, kc_ref, vc_ref, kn_ref, vn_ref, ko_ref, vo_ref):
-    first = start_ref[lax.rem(pl.program_id(0), n_seq)]
+    )(start_pos, x_loc, ln_gain, ln_bias, rope_freqs(head_dim), k_cache, v_cache, w_q, w_k, w_v, w_o, w_up, w_down)
+
+
+def merge_kernel(dims, start_ref, x_ref, kc_ref, vc_ref, kn_ref, vn_ref, xo_ref, ko_ref, vo_ref,
+                 xbuf, kbuf, vbuf, knew, vnew, x_sem, in_sem, new_sem, out_sem):
+    blocks, n_seq, new_len, cache_len, head_dim = dims
     span = new_len + 16
-    base = pl.multiple_of(jnp.minimum(first // 16 * 16, cache_len - span), 16)
-    shift = first - base
-    row = lax.broadcasted_iota(jnp.int32, (span, kc_ref.shape[-1]), 0)
-    inside = jnp.logical_and(row >= shift, row < shift + new_len)
-    for old, new, out in ((kc_ref, kn_ref, ko_ref), (vc_ref, vn_ref, vo_ref)):
-        out[...] = old[...]
-        fresh = new[0].astype(jnp.float32)
-        fresh = jnp.concatenate([fresh, jnp.zeros((16, fresh.shape[-1]), jnp.float32)], axis=0)
-        fresh = pltpu.roll(fresh, shift, 0)
-        kept = old[0, pl.ds(base, span), :].astype(jnp.float32)
-        out[0, pl.ds(base, span), :] = jnp.where(inside, fresh, kept).astype(jnp.bfloat16)
-
-
-def merge_caches(start_pos, k_cache, v_cache, k_new, v_new):
+    row = lax.broadcasted_iota(jnp.int32, (span, head_dim), 0)
+    caches = ((kc_ref, kbuf, kn_ref, knew, ko_ref), (vc_ref, vbuf, vn_ref, vnew, vo_ref))
+
+    def reads(i, c):
+        old, buf, new, nbuf, _ = caches[c]
+        return (pltpu.make_async_copy(old.at[i], buf.at[i], in_sem.at[i, c]),
+                pltpu.make_async_copy(new.at[i], nbuf.at[i], new_sem.at[i, c]))
+
+    def write(i, c):
+        return pltpu.make_async_copy(caches[c][1].at[i], caches[c][4].at[i], out_sem.at[i, c])
+
+    for i in range(blocks):
+        for c in range(2):
+            for copy in reads(i, c):
+                copy.start()
+    x_in = pltpu.make_async_copy(x_ref, xbuf, x_sem.at[0])
+    x_out = pltpu.make_async_copy(xbuf, xo_ref, x_sem.at[1])
+    x_in.start()
+
+    @pl.loop(0, blocks)
+    def _(i):
+        first = start_ref[lax.rem(i, n_seq)]
+        base = pl.multiple_of(jnp.minimum(first // 16 * 16, cache_len - span), 16)
+        shift = first - base
+        inside = jnp.logical_and(row >= shift, row < shift + new_len)
+        for c in range(2):
+            for copy in reads(i, c):
+                copy.wait()
+            _, buf, _, nbuf, _ = caches[c]
+            fresh = jnp.concatenate([nbuf[i].astype(jnp.float32), jnp.zeros((16, head_dim), jnp.float32)], axis=0)
+            fresh = pltpu.roll(fresh, shift, 0)
+            kept = buf[i, pl.ds(base, span), :].astype(jnp.float32)
+            buf[i, pl.ds(base, span), :] = jnp.where(inside, fresh, kept).astype(jnp.bfloat16)
+            write(i, c).start()
+
+    x_in.wait()
+    x_out.start()
+
+    @pl.loop(0, blocks)
+    def _(i):
+        for c in range(2):
+            write(i, c).wait()
+
+    x_out.wait()
+
+
+def merge_caches(start_pos, hidden, k_cache, v_cache, k_new, v_new):
     n_layers, n_seq, kv, cache_len, head_dim = k_cache.shape
     new_len = k_new.shape[2]
     blocks = n_layers * n_seq
+    bf = jnp.bfloat16
     flat = lambda c: c.reshape(blocks, cache_len, head_dim)
-    whole = pl.BlockSpec((1, cache_len, head_dim), lambda i, s: (i, 0, 0))
-    fresh = pl.BlockSpec((1, new_len, head_dim), lambda i, s: (i, 0, 0))
-    shape = jax.ShapeDtypeStruct((blocks, cache_len, head_dim), jnp.bfloat16)
-    k_out, v_out = pl.pallas_call(
-        functools.partial(merge_kernel, new_len, cache_len, n_seq),
-        out_shape=(shape, shape),
-        grid_spec=pltpu.PrefetchScalarGridSpec(num_scalar_prefetch=1, grid=(blocks,), in_specs=[whole, whole, fresh, fresh], out_specs=[whole, whole]),
+    flat_new = lambda c: c.reshape(blocks, new_len, head_dim)
+    hb = pl.BlockSpec(memory_space=pl.ANY)
+    shape = jax.ShapeDtypeStruct((blocks, cache_len, head_dim), bf)
+    dma = pltpu.SemaphoreType.DMA
+    x_out, k_out, v_out = pl.pallas_call(
+        functools.partial(merge_kernel, (blocks, n_seq, new_len, cache_len, head_dim)),
+        out_shape=(jax.ShapeDtypeStruct(hidden.shape, bf), shape, shape),
+        in_specs=[pl.BlockSpec(memory_space=pltpu.SMEM)] + [hb] * 5,
+        out_specs=(hb, hb, hb),
+        scratch_shapes=[pltpu.VMEM(hidden.shape, bf), pltpu.VMEM((blocks, cache_len, head_dim), bf), pltpu.VMEM((blocks, cache_len, head_dim), bf),
+                        pltpu.VMEM((blocks, new_len, head_dim), bf), pltpu.VMEM((blocks, new_len, head_dim), bf),
+                        dma((2,)), dma((blocks, 2)), dma((blocks, 2)), dma((blocks, 2))],
         name='merge',
-    )(start_pos, flat(k_cache), flat(v_cache), k_new.reshape(blocks, new_len, head_dim), v_new.reshape(blocks, new_len, head_dim))
-    return k_out.reshape(k_cache.shape), v_out.reshape(v_cache.shape)
+    )(start_pos, hidden, flat(k_cache), flat(v_cache), flat_new(k_new), flat_new(v_new))
+    return x_out, k_out.reshape(k_cache.shape), v_out.reshape(v_cache.shape)
 
 
 def solution(mesh):
@@ -465,7 +512,6 @@
 
     def device_fn(x_loc, start_pos, k_cache, v_cache, w_q, w_k, w_v, w_o, w_up, w_down, ln_gain, ln_bias):
         hidden, k_new, v_new = run_layers(start_pos, x_loc, k_cache, v_cache, w_q, w_k, w_v, w_o, w_up, w_down, ln_gain, ln_bias, x_loc.shape[1] * tp_size)
-        k_out, v_out = merge_caches(start_pos, k_cache, v_cache, k_new, v_new)
-        return hidden, k_out, v_out
+        return merge_caches(start_pos, hidden, k_cache, v_cache, k_new, v_new)
 
     return jax.shard_map(device_fn, mesh=mesh, in_specs=(tok_spec, P('dp'), cache_spec, cache_spec, col_spec, col_spec, col_spec, row_spec, col_spec, row_spec, P(), P()), out_specs=(tok_spec, cache_spec, cache_spec), check_vma=False)

time: 352 us -> 285 us (0.81)
  Pallas kernels: 342 us -> 283 us
  other arithmetic: 5.33 us -> 0.01 us
    pallas_call x1, Pallas kernels: 332 us -> 273 us  [run_layers(): pl.pallas_call(functools.partial(layers_kernel, dims), out_shape=(jax.Sha...]
where the time goes in v2:
time: 285 us; the launch traced here: 284 us
  Pallas kernels  283 us (99%)
    pallas_call x1, Pallas kernels, run_layers(): pl.pallas_call(functools.partial(layers_kernel, dims), out_shape=(jax.Sha...  273 us
    pallas_call x1, Pallas kernels, merge_caches(): pl.pallas_call(functools.partial(merge_kernel, (blocks, n_seq, new_len, c...  9.92 us

profile of v2, /device:TPU:81, one launch (start us, length us, event | category | flops | bytes accessed | tf_op | source)
XLA Modules:
  0.0 284.4 jit_solution(14591307618459010445)
XLA Ops:
  0.7 0.6 broadcast_in_dim_tile.3.freq_ref
  1.2 273.3 %layers.1 = (bf16[3,48,3072]{2,1,0:T(8,128)(2,1)}, bf16[2,3,384,128]{3,2,1,0:T(8,128)(2,1)}, bf16[2,3,384,128]{3,2,1,0:T(8,128)(2,1)}) custom-call(s32[3]{0:T(128)} %start_ref.3, bf16[3,48,3072]{2,1,0:T(8,128)(2,1)} %x_ref.1, bf16[2,2,3072]{2,1,0:T(2,128)(2,1)} %lng_ref.1, bf16[2,2,3072]{2,1,0:T(2,128)(2,1)} %lnb_ref.1, ...), custom_call_target="tpu_custom_call" | custom-call | tf_op jit(solution)/shard_map/layers/pallas_call | solution.py:394
  274.5 9.9 %merge.1 = (bf16[3,48,3072]{2,1,0:T(8,128)(2,1)}, bf16[6,3456,128]{2,1,0:T(8,128)(2,1)}, bf16[6,3456,128]{2,1,0:T(8,128)(2,1)}) custom-call(s32[3]{0:T(128)} %start_ref.3, bf16[3,48,3072]{2,1,0:T(8,128)(2,1)} %get-tuple-element.9.x_ref, bf16[6,3456,128]{2,1,0:T(8,128)(2,1)} %bitcast.10, bf16[6,3456,128]{2,1,0:T(8,128)(2,1)} %bitcast.11, ...), custom_call_target="tpu_custom_call" | custom-call | tf_op jit(solution)/shard_map/merge/pallas_call | solution.py:492
  (2 shorter events, 0.0 us)

commit v3 on v2

--- a/solution.py
+++ b/solution.py
@@ -3,6 +3,7 @@
 
 import jax
 import jax.numpy as jnp
+import numpy as np
 from jax import lax
 from jax.experimental import pallas as pl
 from jax.experimental.pallas import tpu as pltpu
@@ -19,14 +20,14 @@
 def rope_freqs(head_dim):
     rot_dim = head_dim // 2
     half_rot = rot_dim // 2
-    inv_freq = ROPE_BASE ** (-(jnp.arange(half_rot, dtype=jnp.float32) * (2.0 / rot_dim)))
-    return jnp.tile(inv_freq, head_dim // half_rot)[None]
+    inv_freq = ROPE_BASE ** (-(np.arange(half_rot) * (2.0 / rot_dim)))
+    return jnp.asarray(np.tile(inv_freq, head_dim // half_rot)[None].astype(np.float32))
 
 
 def layers_kernel(dims, start_ref, x_ref, lng_ref, lnb_ref, freq_ref, kc_ref, vc_ref,
                   wq_ref, wk_ref, wv_ref, wo_ref, wu_ref, wd_ref,
                   xo_ref, kn_ref, vn_ref,
-                  gath, part, pairin, pair, d2in, fin, wqkv, wov, wuv, wdv, kbuf, vbuf, qbuf, cbuf, abuf, sbuf_a, sbuf_b,
+                  gath, part, pairin, pair, d2in, fin, wqkv, wov, wuv, wdv, kbuf, vbuf, abuf, sbuf_a, sbuf_b,
                   gain_ref, bias_ref, cos_ref, slo_ref, shi_ref,
                   ag_s, ag_r, dd_s, dd_r, d2_s, d2_r, f_s, f_r, w_sem, kv_sem, kn_sem):
     n_layers, n_seq, tok, d_model, heads, head_dim, prefix, ff = dims
@@ -68,9 +69,10 @@
         for k in ks:
             ag_copy(m, k).wait_recv()
 
-    def dd_copy(k):
+    def dd_copy(n, k):
+        p = n % 2
         cols = (lo, hi)[k]
-        return remote(part.at[:, sib, :, cols], pairin.at[:, :, cols], dd_s.at[k], dd_r.at[k], sibling)
+        return remote(part.at[:, sib, :, cols], pairin.at[p, :, :, cols], dd_s.at[p, k], dd_r.at[p, k], sibling)
 
     def d2_copy(n, k):
         p = n % 2
@@ -116,30 +118,33 @@
         out = cen * lax.rsqrt(var + LN_EPS) * gain_ref[idx] + bias_ref[idx]
         gath[m % GSLOTS, chip, core] = out.astype(jnp.bfloat16)
 
-    def pair_sum(n):
-        for k in range(11):
-            ag_copy(n, k).wait_send()
-
-        @pl.when(n >= 2)
-        def _():
-            for k in range(2):
-                d2_copy(n - 2, k).wait_send()
-            for k in range(4):
-                f_copy(n - 2, k).wait_send()
+    def pair_sum(n, k):
+        if k == 0:
+            for i in range(11):
+                ag_copy(n, i).wait_send()
+
+            @pl.when(n >= 2)
+            def _():
+                for i in range(2):
+                    d2_copy(n - 2, i).wait_send()
+                for i in range(4):
+                    f_copy(n - 2, i).wait_send()
 
         p = n % 2
-
-        def add(c, cols):
-            pair[p, c, :, cols] = (part[c, core, :, cols].astype(jnp.float32) + pairin[c, :, cols].astype(jnp.float32)).astype(jnp.bfloat16)
-
-        for k, (cols, near, ready, far) in enumerate(((lo, lchip, 2, rchip), (hi, rchip, 0, lchip))):
-            dd_copy(k).wait()
-            add(ochip, cols)
-            d2_copy(n, k).start()
-            add(near, cols)
-            f_copy(n, ready).start()
-            add(far, cols)
-            add(chip, cols)
+        cols, near, far = ((lo, lchip, rchip), (hi, rchip, lchip))[k]
+
+        def add(c):
+            pair[p, c, :, cols] = (part[c, core, :, cols].astype(jnp.float32) + pairin[p, c, :, cols].astype(jnp.float32)).astype(jnp.bfloat16)
+
+        dd_copy(n, k).wait()
+        add(ochip)
+        d2_copy(n, k).start()
+        add(near)
+        add(far)
+        if k == 1:
+            f_copy(n, 0).start()
+            f_copy(n, 2).start()
+        add(chip)
 
     def add_through(n):
         p = n % 2
@@ -160,11 +165,13 @@
         o = o.astype(jnp.bfloat16).astype(jnp.float32)
         xo_ref[b] = (xo_ref[b].astype(jnp.float32) + o).astype(jnp.bfloat16)
 
-    def forward(m):
+    def forward_on(m):
         ag_wait_recv(m, (0,))
         ag_start(m, (5,))
         ag_wait_recv(m, (2,))
         ag_start(m, (6,))
+
+    def forward_sib(m):
         ag_wait_recv(m, (1,))
         ag_start(m, (7,))
         ag_wait_recv(m, (3,))
@@ -187,11 +194,19 @@
     def event_forward(n):
         @pl.when(n + 1 < steps)
         def _():
-            forward(n + 1)
-
-    def after_compute(n):
-        pair_sum(n)
-
+            forward_on(n + 1)
+
+    def event_sib(n):
+        @pl.when(n + 1 < steps)
+        def _():
+            forward_sib(n + 1)
+
+    def event_far(n):
+        @pl.when(n + 1 < steps)
+        def _():
+            forward_far(n + 1)
+
+    def event_finalize(n):
         @pl.when(n >= 1)
         def _():
             finalize(n - 1)
@@ -201,9 +216,12 @@
                 norm_into((n + 2) % n_seq, (n + 2) // n_seq, n + 2)
                 ag_start(n + 2, range(5))
 
-        @pl.when(n + 1 < steps)
-        def _():
-            forward_far(n + 1)
+    def after_compute(n):
+        pair_sum(n, 0)
+        event_sib(n)
+        pair_sum(n, 1)
+        event_finalize(n)
+        event_far(n)
 
     def rows_of(g):
         return gath[g].reshape(new_len, d_model)
@@ -214,14 +232,15 @@
     NT = (((1,), (1,)), ((), ()))
     tile = 256
 
-    def product_into_part(lhs, weights):
-        for k in range(2):
-            @pl.loop(0, half // tile)
-            def _(j):
-                cols = pl.ds(pl.multiple_of(k * half + j * tile, tile), tile)
-                put_part(cols, jnp.dot(lhs[...], weights[:, cols], preferred_element_type=jnp.float32))
-
-            dd_copy(k).start()
+    def product_into_part(n, c0, width, weights, between):
+        quarter = half // 2
+        for k in range(4):
+            if k == 1:
+                between(n)
+            cols = pl.ds(k * quarter, quarter)
+            put_part(cols, jnp.dot(abuf[:, pl.ds(c0, width)], weights[:, cols], preferred_element_type=jnp.float32))
+            if k % 2:
+                dd_copy(n, k // 2).start()
 
     def attn_step(l, b, n):
         a = l * n_seq + b
@@ -250,10 +269,10 @@
         @pl.loop(0, heads // 2)
         def _(j):
             q2 = jnp.dot(rows_of(g), wqkv[:, pl.ds(pl.multiple_of(j * tile, tile), tile)], preferred_element_type=jnp.float32)
-            qbuf[2 * j] = rotate(q2[:, :head_dim])
-            qbuf[2 * j + 1] = rotate(q2[:, head_dim:])
-
-        event_add(n)
+            base = pl.multiple_of(j * tile, tile)
+            abuf[:, pl.ds(base, head_dim)] = rotate(q2[:, :head_dim])
+            abuf[:, pl.ds(base + head_dim, head_dim)] = rotate(q2[:, head_dim:])
+
         first_len = start_ref[b]
         chunk = prefix // 4
         chunks = [(c, chunk) for c in range(0, prefix, chunk)] + [(prefix, new_len)]
@@ -283,9 +302,11 @@
 
         peaks = None
         for h in range(heads + 1):
+            if h == heads // 2:
+                event_add(n)
             if h == heads:
                 event_forward(n)
-            q = qbuf[h] if h < heads else None
+            q = abuf[:, pl.ds(h * head_dim, head_dim)] if h < heads else None
             next_peak = total = acc = None
             for c0, cl in chunks:
                 if h < heads:
@@ -294,11 +315,11 @@
                     total, acc = weigh_chunk(h - 1, peaks, total, acc, c0, cl)
             if h:
                 ctx = acc / jnp.sum(total, axis=-1, keepdims=True)
-                cbuf[:, pl.ds((h - 1) * head_dim, head_dim)] = ctx.astype(jnp.bfloat16)
+                abuf[:, pl.ds((heads + h - 1) * head_dim, head_dim)] = ctx.astype(jnp.bfloat16)
             if h < heads:
                 peaks = jnp.max(next_peak, axis=-1, keepdims=True)
 
-        product_into_part(cbuf, wov)
+        product_into_part(n, heads * head_dim, heads * head_dim, wov, lambda n: None)
         wait(outs)
         after_compute(n)
 
@@ -318,25 +339,29 @@
         if ff % tile:
             up(pl.ds(ff - ff % tile, ff % tile))
         event_add(n)
-        product_into_part(abuf, wdv)
-        event_forward(n)
+        product_into_part(n, 0, ff, wdv, event_forward)
         after_compute(n)
 
-    start(attn_weights(0))
-    start(kv_loads(0))
-    xo_ref[...] = x_ref[...]
-    for l in range(n_layers):
-        for k in range(2):
-            gain_ref[2 * l + k] = 1.0 + lng_ref[l, k:k + 1].astype(jnp.float32)
-            bias_ref[2 * l + k] = lnb_ref[l, k:k + 1].astype(jnp.float32)
+    def affine(l, k):
+        gain_ref[2 * l + k] = 1.0 + lng_ref[l, k:k + 1].astype(jnp.float32)
+        bias_ref[2 * l + k] = lnb_ref[l, k:k + 1].astype(jnp.float32)
 
     barrier = pltpu.get_barrier_semaphore()
     for dev in (left, right, sibling):
         pl.semaphore_signal(barrier, inc=1, device_id=dev, device_id_type=pl.DeviceIdType.MESH)
+    start(attn_weights(0))
+    start(kv_loads(0))
+    affine(0, 0)
+    xo_ref[0] = x_ref[0]
+    norm_into(0, 0, 0)
     pl.semaphore_wait(barrier, 3)
-    for b in range(n_seq):
+    ag_start(0, range(5))
+    for b in range(1, n_seq):
+        xo_ref[b] = x_ref[b]
         norm_into(b, 0, b)
-        ag_start(b, range(5))
+    for i in range(1, 2 * n_layers):
+        affine(i // 2, i % 2)
+
     lane = lax.broadcasted_iota(jnp.int32, (new_len, head_dim), 1)
     row = lax.broadcasted_iota(jnp.int32, (new_len, head_dim), 0)
     rot = head_dim // 2
@@ -349,7 +374,10 @@
         slo_ref[b] = jnp.where(lane < rot // 2, -sin_a, 0.0)
         shi_ref[b] = jnp.where(jnp.logical_and(lane >= rot // 2, lane < rot), sin_a, 0.0)
 
-    forward(0)
+    forward_on(0)
+    ag_start(1, range(5))
+    forward_sib(0)
+    ag_start(2, range(5))
     forward_far(0)
 
     @pl.loop(0, n_layers)
@@ -401,7 +429,7 @@
         scratch_shapes=[
             pltpu.VMEM((GSLOTS, CHIPS, CORES, tok, d_model), bf),
             pltpu.VMEM((CHIPS, CORES, tok, d_model), bf),
-            pltpu.VMEM((CHIPS, tok, d_model), bf),
+            pltpu.VMEM((2, CHIPS, tok, d_model), bf),
             pltpu.VMEM((2, CHIPS, tok, d_model), bf),
             pltpu.VMEM((2, 2, tok, d_model // 2), bf),
             pltpu.VMEM((3, 2, tok, d_model), bf),
@@ -411,9 +439,7 @@
             pltpu.VMEM((ff, d_model), bf),
             pltpu.VMEM((2, cache_len, head_dim), bf),
             pltpu.VMEM((2, cache_len, head_dim), bf),
-            pltpu.VMEM((heads, new_len, head_dim), bf),
-            pltpu.VMEM((new_len, heads * head_dim), bf),
-            pltpu.VMEM((new_len, ff), bf),
+            pltpu.VMEM((new_len, max(ff, 2 * heads * head_dim)), bf),
             pltpu.VMEM((new_len, cache_len), f32),
             pltpu.VMEM((new_len, cache_len), f32),
             pltpu.VMEM((n_layers * 2, 1, d_model), f32),
@@ -421,7 +447,7 @@
             pltpu.VMEM((n_seq, new_len, head_dim), f32),
             pltpu.VMEM((n_seq, new_len, head_dim), f32),
             pltpu.VMEM((n_seq, new_len, head_dim), f32),
-            dma((GSLOTS, 11)), dma((GSLOTS, 11)), dma((2,)), dma((2,)), dma((2, 2)), dma((2, 2)), dma((3, 4)), dma((3, 4)),
+            dma((GSLOTS, 11)), dma((GSLOTS, 11)), dma((2, 2)), dma((2, 2)), dma((2, 2)), dma((2, 2)), dma((3, 4)), dma((3, 4)),
             dma((6,)), dma((2, 2)), dma((2,)),
         ],
         compiler_params=pltpu.CompilerParams(collective_id=0, has_side_effects=True, vmem_limit_bytes=67043328),

time: 285 us -> 259 us (0.909)
  Pallas kernels: 283 us -> 258 us
    pallas_call x1, Pallas kernels: 273 us -> 248 us  [run_layers(): pl.pallas_call(functools.partial(layers_kernel, dims), out_shape=(jax.Sha...]
where the time goes in v3:
time: 259 us
  Pallas kernels  258 us (100%)
    pallas_call x1, Pallas kernels, run_layers(): pl.pallas_call(functools.partial(layers_kernel, dims), out_shape=(jax.Sha...  248 us
    pallas_call x1, Pallas kernels, merge_caches(): pl.pallas_call(functools.partial(merge_kernel, (blocks, n_seq, new_len, c...  9.92 us

profile of v3, /device:TPU:81, one launch (start us, length us, event | category | flops | bytes accessed | tf_op | source)
XLA Modules:
  0.0 258.9 jit_solution(13626622925798403713)
XLA Ops:
  0.6 248.1 %layers.1 = (bf16[3,48,3072]{2,1,0:T(8,128)(2,1)}, bf16[2,3,384,128]{3,2,1,0:T(8,128)(2,1)}, bf16[2,3,384,128]{3,2,1,0:T(8,128)(2,1)}) custom-call(s32[3]{0:T(128)} %start_ref.3, bf16[3,48,3072]{2,1,0:T(8,128)(2,1)} %x_ref.1, bf16[2,2,3072]{2,1,0:T(2,128)(2,1)} %lng_ref.1, bf16[2,2,3072]{2,1,0:T(2,128)(2,1)} %lnb_ref.1, f32[1,128]{1,0:T(1,128)} %constant.2.clone.freq_ref, ...), custom_call_target="tpu_custom_call" | custom-call | tf_op jit(solution)/shard_map/layers/pallas_call | solution.py:422
  248.8 9.9 %merge.1 = (bf16[3,48,3072]{2,1,0:T(8,128)(2,1)}, bf16[6,3456,128]{2,1,0:T(8,128)(2,1)}, bf16[6,3456,128]{2,1,0:T(8,128)(2,1)}) custom-call(s32[3]{0:T(128)} %start_ref.3, bf16[3,48,3072]{2,1,0:T(8,128)(2,1)} %get-tuple-element.9.x_ref, bf16[6,3456,128]{2,1,0:T(8,128)(2,1)} %bitcast.10, bf16[6,3456,128]{2,1,0:T(8,128)(2,1)} %bitcast.11, ...), custom_call_target="tpu_custom_call" | custom-call | tf_op jit(solution)/shard_map/merge/pallas_call | solution.py:518

commit v4 on v3

--- a/solution.py
+++ b/solution.py
@@ -28,7 +28,7 @@
                   wq_ref, wk_ref, wv_ref, wo_ref, wu_ref, wd_ref,
                   xo_ref, kn_ref, vn_ref,
                   gath, part, pairin, pair, d2in, fin, wqkv, wov, wuv, wdv, kbuf, vbuf, abuf, sbuf_a, sbuf_b,
-                  gain_ref, bias_ref, cos_ref, slo_ref, shi_ref,
+                  gain_ref, bias_ref, cos_ref, sin_ref,
                   ag_s, ag_r, dd_s, dd_r, d2_s, d2_r, f_s, f_r, w_sem, kv_sem, kn_sem):
     n_layers, n_seq, tok, d_model, heads, head_dim, prefix, ff = dims
     new_len = tok * CORES * CHIPS
@@ -118,6 +118,10 @@
         out = cen * lax.rsqrt(var + LN_EPS) * gain_ref[idx] + bias_ref[idx]
         gath[m % GSLOTS, chip, core] = out.astype(jnp.bfloat16)
 
+    def ready_start(n):
+        f_copy(n, 0).start()
+        f_copy(n, 2).start()
+
     def pair_sum(n, k):
         if k == 0:
             for i in range(11):
@@ -142,17 +146,18 @@
         add(near)
         add(far)
         if k == 1:
-            f_copy(n, 0).start()
-            f_copy(n, 2).start()
+            @pl.when(jnp.logical_or(n < last_gather, n == steps - 1))
+            def _():
+                ready_start(n)
+
         add(chip)
 
     def add_through(n):
         p = n % 2
-        d2_copy(n, 0).wait_recv()
-        pair[p, rchip, :, lo] = (pair[p, rchip, :, lo].astype(jnp.float32) + d2in[p, 0].astype(jnp.float32)).astype(jnp.bfloat16)
+        for k, c, cols in ((0, rchip, lo), (1, lchip, hi)):
+            d2_copy(n, k).wait_recv()
+            pair[p, c, :, cols] = (pair[p, c, :, cols].astype(jnp.float32) + d2in[p, k].astype(jnp.float32)).astype(jnp.bfloat16)
         f_copy(n, 1).start()
-        d2_copy(n, 1).wait_recv()
-        pair[p, lchip, :, hi] = (pair[p, lchip, :, hi].astype(jnp.float32) + d2in[p, 1].astype(jnp.float32)).astype(jnp.bfloat16)
         f_copy(n, 3).start()
 
     def finalize(n):
@@ -186,8 +191,10 @@
     def gathered(n):
         ag_wait_recv(n, (4, 7, 8, 9, 10))
 
+    last_gather = steps - 3
+
     def event_add(n):
-        @pl.when(n >= 1)
+        @pl.when(jnp.logical_and(n >= 1, n <= last_gather))
         def _():
             add_through(n - 1)
 
@@ -217,11 +224,42 @@
                 ag_start(n + 2, range(5))
 
     def after_compute(n):
+        early = n <= n_seq - 2
+
+        @pl.when(n == steps - 1)
+        def _():
+            add_through(n - 1)
+            finalize(last_gather)
+
         pair_sum(n, 0)
-        event_sib(n)
+
+        @pl.when(early)
+        def _():
+            event_far(n)
+
+        @pl.when(jnp.logical_not(early))
+        def _():
+            event_sib(n)
+
+        @pl.when(n == last_gather + 1)
+        def _():
+            ready_start(last_gather)
+            add_through(last_gather)
+
         pair_sum(n, 1)
-        event_finalize(n)
-        event_far(n)
+
+        @pl.when(n == last_gather + 1)
+        def _():
+            event_far(n)
+            ready_start(n)
+
+        @pl.when(n != last_gather + 1)
+        def _():
+            event_finalize(n)
+
+            @pl.when(jnp.logical_not(early))
+            def _():
+                event_far(n)
 
     def rows_of(g):
         return gath[g].reshape(new_len, d_model)
@@ -242,6 +280,25 @@
             if k % 2:
                 dd_copy(n, k // 2).start()
 
+    def qkv(b, p, g):
+        quarter = head_dim // 4
+        lane = lax.broadcasted_iota(jnp.int32, (new_len, head_dim), 1)
+
+        def rotate(val):
+            other = jnp.where(lane < quarter, pltpu.roll(val, head_dim - quarter, 1), pltpu.roll(val, quarter, 1))
+            return (val * cos_ref[b] + other * sin_ref[b]).astype(jnp.bfloat16)
+
+        kv = jnp.dot(rows_of(g), wqkv[:, pl.ds(heads * head_dim, 2 * head_dim)], preferred_element_type=jnp.float32)
+        kbuf[p, pl.ds(prefix, new_len)] = rotate(kv[:, :head_dim])
+        vbuf[p, pl.ds(prefix, new_len)] = kv[:, head_dim:].astype(jnp.bfloat16)
+
+        @pl.loop(0, heads // 2)
+        def _(j):
+            base = pl.multiple_of(j * tile, tile)
+            q2 = jnp.dot(rows_of(g), wqkv[:, pl.ds(base, tile)], preferred_element_type=jnp.float32)
+            abuf[:, pl.ds(base, head_dim)] = rotate(q2[:, :head_dim])
+            abuf[:, pl.ds(base + head_dim, head_dim)] = rotate(q2[:, head_dim:])
+
     def attn_step(l, b, n):
         a = l * n_seq + b
         p = a % 2
@@ -252,27 +309,12 @@
             start(kv_loads(a + 1))
 
         gathered(n)
-        g = n % GSLOTS
-        cos_t, sin_lo, sin_hi = cos_ref[b], slo_ref[b], shi_ref[b]
-        quarter = head_dim // 4
-
-        def rotate(val):
-            return (val * cos_t + pltpu.roll(val, head_dim - quarter, 1) * sin_lo + pltpu.roll(val, quarter, 1) * sin_hi).astype(jnp.bfloat16)
-
-        kv = jnp.dot(rows_of(g), wqkv[:, pl.ds(heads * head_dim, 2 * head_dim)], preferred_element_type=jnp.float32)
-        kbuf[p, pl.ds(prefix, new_len)] = rotate(kv[:, :head_dim])
-        vbuf[p, pl.ds(prefix, new_len)] = kv[:, head_dim:].astype(jnp.bfloat16)
+        qkv(b, p, n % GSLOTS)
         outs = [pltpu.make_async_copy(kbuf.at[p, pl.ds(prefix, new_len)], kn_ref.at[l, b], kn_sem.at[0]),
                 pltpu.make_async_copy(vbuf.at[p, pl.ds(prefix, new_len)], vn_ref.at[l, b], kn_sem.at[1])]
         start(outs)
 
-        @pl.loop(0, heads // 2)
-        def _(j):
-            q2 = jnp.dot(rows_of(g), wqkv[:, pl.ds(pl.multiple_of(j * tile, tile), tile)], preferred_element_type=jnp.float32)
-            base = pl.multiple_of(j * tile, tile)
-            abuf[:, pl.ds(base, head_dim)] = rotate(q2[:, :head_dim])
-            abuf[:, pl.ds(base + head_dim, head_dim)] = rotate(q2[:, head_dim:])
-
+        early = n <= n_seq - 2
         first_len = start_ref[b]
         chunk = prefix // 4
         chunks = [(c, chunk) for c in range(0, prefix, chunk)] + [(prefix, new_len)]
@@ -302,10 +344,13 @@
 
         peaks = None
         for h in range(heads + 1):
+            if h == 1:
+                pl.when(early)(lambda: event_forward(n))
             if h == heads // 2:
                 event_add(n)
+                pl.when(early)(lambda: event_sib(n))
             if h == heads:
-                event_forward(n)
+                pl.when(jnp.logical_not(early))(lambda: event_forward(n))
             q = abuf[:, pl.ds(h * head_dim, head_dim)] if h < heads else None
             next_peak = total = acc = None
             for c0, cl in chunks:
@@ -371,8 +416,7 @@
         angle = (start_ref[b] + row).astype(jnp.float32) * freq_ref[...]
         sin_a = jnp.sin(angle)
         cos_ref[b] = jnp.where(lane < rot, jnp.cos(angle), 1.0)
-        slo_ref[b] = jnp.where(lane < rot // 2, -sin_a, 0.0)
-        shi_ref[b] = jnp.where(jnp.logical_and(lane >= rot // 2, lane < rot), sin_a, 0.0)
+        sin_ref[b] = jnp.where(lane < rot // 2, -sin_a, jnp.where(lane < rot, sin_a, 0.0))
 
     forward_on(0)
     ag_start(1, range(5))
@@ -446,7 +490,6 @@
             pltpu.VMEM((n_layers * 2, 1, d_model), f32),
             pltpu.VMEM((n_seq, new_len, head_dim), f32),
             pltpu.VMEM((n_seq, new_len, head_dim), f32),
-            pltpu.VMEM((n_seq, new_len, head_dim), f32),
             dma((GSLOTS, 11)), dma((GSLOTS, 11)), dma((2, 2)), dma((2, 2)), dma((2, 2)), dma((2, 2)), dma((3, 4)), dma((3, 4)),
             dma((6,)), dma((2, 2)), dma((2,)),
         ],

time: 259 us -> 255 us (0.985)
  Pallas kernels: 258 us -> 254 us
    pallas_call x1, Pallas kernels: 248 us -> 244 us  [run_layers(): pl.pallas_call(functools.partial(layers_kernel, dims), out_shape=(jax.Sha...]
where the time goes in v4:
time: 255 us
  Pallas kernels  254 us (100%)
    pallas_call x1, Pallas kernels, run_layers(): pl.pallas_call(functools.partial(layers_kernel, dims), out_shape=(jax.Sha...  244 us
    pallas_call x1, Pallas kernels, merge_caches(): pl.pallas_call(functools.partial(merge_kernel, (blocks, n_seq, new_len, c...  9.92 us

profile of v4, /device:TPU:81, one launch (start us, length us, event | category | flops | bytes accessed | tf_op | source)
XLA Modules:
  0.0 254.9 jit_solution(15348369020247352026)
XLA Ops:
  0.6 244.2 %layers.1 = (bf16[3,48,3072]{2,1,0:T(8,128)(2,1)}, bf16[2,3,384,128]{3,2,1,0:T(8,128)(2,1)}, bf16[2,3,384,128]{3,2,1,0:T(8,128)(2,1)}) custom-call(s32[3]{0:T(128)} %start_ref.3, bf16[3,48,3072]{2,1,0:T(8,128)(2,1)} %x_ref.1, bf16[2,2,3072]{2,1,0:T(2,128)(2,1)} %lng_ref.1, bf16[2,2,3072]{2,1,0:T(2,128)(2,1)} %lnb_ref.1, f32[1,128]{1,0:T(1,128)} %constant.2.clone.freq_ref, ...), custom_call_target="tpu_custom_call" | custom-call | tf_op jit(solution)/shard_map/layers/pallas_call | solution.py:466
  244.8 9.9 %merge.1 = (bf16[3,48,3072]{2,1,0:T(8,128)(2,1)}, bf16[6,3456,128]{2,1,0:T(8,128)(2,1)}, bf16[6,3456,128]{2,1,0:T(8,128)(2,1)}) custom-call(s32[3]{0:T(128)} %start_ref.3, bf16[3,48,3072]{2,1,0:T(8,128)(2,1)} %get-tuple-element.9.x_ref, bf16[6,3456,128]{2,1,0:T(8,128)(2,1)} %bitcast.10, bf16[6,3456,128]{2,1,0:T(8,128)(2,1)} %bitcast.11, ...), custom_call_target="tpu_custom_call" | custom-call | tf_op jit(solution)/shard_map/merge/pallas_call | solution.py:561

commit v5 on v4

--- a/solution.py
+++ b/solution.py
@@ -292,9 +292,7 @@
         kbuf[p, pl.ds(prefix, new_len)] = rotate(kv[:, :head_dim])
         vbuf[p, pl.ds(prefix, new_len)] = kv[:, head_dim:].astype(jnp.bfloat16)
 
-        @pl.loop(0, heads // 2)
-        def _(j):
-            base = pl.multiple_of(j * tile, tile)
+        for base in range(0, heads * head_dim, tile):
             q2 = jnp.dot(rows_of(g), wqkv[:, pl.ds(base, tile)], preferred_element_type=jnp.float32)
             abuf[:, pl.ds(base, head_dim)] = rotate(q2[:, :head_dim])
             abuf[:, pl.ds(base + head_dim, head_dim)] = rotate(q2[:, head_dim:])
@@ -377,12 +375,9 @@
             val = jnp.maximum(val, 0.0)
             abuf[:, cols] = (val * val).astype(jnp.bfloat16)
 
-        @pl.loop(0, ff // tile)
-        def _(j):
-            up(pl.ds(pl.multiple_of(j * tile, tile), tile))
-
-        if ff % tile:
-            up(pl.ds(ff - ff % tile, ff % tile))
+        for c0 in range(0, ff, 2 * tile):
+            up(pl.ds(c0, min(2 * tile, ff - c0)))
+
         event_add(n)
         product_into_part(n, 0, ff, wdv, event_forward)
         after_compute(n)

time: 255 us -> 253 us (level)
  no operation moved by 1% of the time
where the time goes in v5:
time: 253 us
  Pallas kernels  252 us (100%)
    pallas_call x1, Pallas kernels, run_layers(): pl.pallas_call(functools.partial(layers_kernel, dims), out_shape=(jax.Sha...  242 us
    pallas_call x1, Pallas kernels, merge_caches(): pl.pallas_call(functools.partial(merge_kernel, (blocks, n_seq, new_len, c...  9.92 us

profile of v5, /device:TPU:81, one launch (start us, length us, event | category | flops | bytes accessed | tf_op | source)
XLA Modules:
  0.0 252.7 jit_solution(17790540899523443826)
XLA Ops:
  0.6 242.0 %layers.1 = (bf16[3,48,3072]{2,1,0:T(8,128)(2,1)}, bf16[2,3,384,128]{3,2,1,0:T(8,128)(2,1)}, bf16[2,3,384,128]{3,2,1,0:T(8,128)(2,1)}) custom-call(s32[3]{0:T(128)} %start_ref.3, bf16[3,48,3072]{2,1,0:T(8,128)(2,1)} %x_ref.1, bf16[2,2,3072]{2,1,0:T(2,128)(2,1)} %lng_ref.1, bf16[2,2,3072]{2,1,0:T(2,128)(2,1)} %lnb_ref.1, f32[1,128]{1,0:T(1,128)} %constant.2.clone.freq_ref, ...), custom_call_target="tpu_custom_call" | custom-call | tf_op jit(solution)/shard_map/layers/pallas_call | solution.py:461
  242.6 9.9 %merge.1 = (bf16[3,48,3072]{2,1,0:T(8,128)(2,1)}, bf16[6,3456,128]{2,1,0:T(8,128)(2,1)}, bf16[6,3456,128]{2,1,0:T(8,128)(2,1)}) custom-call(s32[3]{0:T(128)} %start_ref.3, bf16[3,48,3072]{2,1,0:T(8,128)(2,1)} %get-tuple-element.9.x_ref, bf16[6,3456,128]{2,1,0:T(8,128)(2,1)} %bitcast.10, bf16[6,3456,128]{2,1,0:T(8,128)(2,1)} %bitcast.11, ...), custom_call_target="tpu_custom_call" | custom-call | tf_op jit(solution)/shard_map/merge/pallas_call | solution.py:556
